TPU v7x, 128 devices: a whole 4x4x4 slice. The times are simulated.
128 devices in a mesh: model: 1, data: 128 (over z, y, x, core).
Axes of the slice: x: 4, y: 4, z: 4, core: 2. Of those that a mesh axis runs over, the one named last changes fastest.
Arguments:
- grad_sq: float32 [128, 2, 896, 896], P(('model', 'data'))
- mom_sq: float32 [2, 896, 896], P('model', 'data')
- weight_sq: float32 [2, 896, 896], P('model', 'data')
- grad_kv: float32 [128, 2, 896, 64], P(('model', 'data'))
- mom_kv: float32 [2, 896, 64], P('model', 'data')
- weight_kv: float32 [2, 896, 64], P('model', 'data')
- grad_up: float32 [128, 2, 896, 256], P(('model', 'data'))
- mom_up: float32 [2, 896, 256], P('model', 'data')
- weight_up: float32 [2, 896, 256], P('model', 'data')
- grad_down: float32 [128, 1, 256, 896], P(('model', 'data'))
- mom_down: float32 [1, 256, 896], P('model', 'data')
- weight_down: float32 [1, 256, 896], P('model', 'data')
Outputs:
- output 1: float32 [2, 896, 896], P('model', 'data')
- output 2: float32 [2, 896, 896], P('model', 'data')
- output 3: bfloat16 [2, 896, 896], P('model')
- output 4: float32 [2, 896, 64], P('model', 'data')
- output 5: float32 [2, 896, 64], P('model', 'data')
- output 6: bfloat16 [2, 896, 64], P('model')
- output 7: float32 [2, 896, 256], P('model', 'data')
- output 8: float32 [2, 896, 256], P('model', 'data')
- output 9: bfloat16 [2, 896, 256], P('model')
- output 10: float32 [1, 256, 896], P('model', 'data')
- output 11: float32 [1, 256, 896], P('model', 'data')
- output 12: bfloat16 [1, 256, 896], P('model')
All inputs are finite; a program needn't handle non-finite values.
Results may differ from a plain program's by a relative error of at most 0.0103988.
Values are sent between devices in bfloat16 or wider.
A program may use at most 1 GiB of HBM per device.

v0:
```python
import math
import jax
import jax.numpy as jnp
from jax import lax
from jax.sharding import PartitionSpec as P, NamedSharding

NS_STEPS = 5
MU = 0.95
LR = 0.1
WD = 0.5
EPS = 1e-7
COEF_A = 3.4445
COEF_B = -4.7750
COEF_C = 2.0315


def orthogonalize(update):
    rows, columns = update.shape[1], update.shape[2]
    update_f32 = update.astype(jnp.float32)
    frob_norm = jnp.sqrt(jnp.sum(update_f32 * update_f32, axis=(1, 2), keepdims=True))
    ortho = (update_f32 / (frob_norm + EPS)).astype(jnp.bfloat16)
    if rows > columns:
        gram_form = "bmk,bmj->bkj"
        apply_form = "bkj,bmj->bmk"
    else:
        gram_form = "bkm,bjm->bkj"
        apply_form = "bkj,bjm->bkm"
    for step_index in range(NS_STEPS):
        gram_mat = jnp.einsum(gram_form, ortho, ortho, preferred_element_type=jnp.float32).astype(jnp.bfloat16)
        square = jnp.einsum("bki,bij->bkj", gram_mat, gram_mat, preferred_element_type=jnp.float32)
        poly_mat = (COEF_B * gram_mat.astype(jnp.float32) + COEF_C * square).astype(jnp.bfloat16)
        ortho = (COEF_A * ortho.astype(jnp.float32) + jnp.einsum(apply_form, poly_mat, ortho, preferred_element_type=jnp.float32)).astype(jnp.bfloat16)
    return ortho


def family_local(grad_part, momentum, weight, group_size):
    count, local_rows, columns = momentum.shape
    rows = local_rows * group_size
    summed = lax.psum_scatter(grad_part[0], "data", scatter_dimension=1, tiled=True) / group_size
    mom_new = MU * momentum + summed
    update = (summed + MU * mom_new).astype(jnp.bfloat16)
    rounds = (count + group_size - 1) // group_size
    filled = jnp.pad(update, ((0, rounds * group_size - count), (0, 0), (0, 0)))
    owned = lax.all_to_all(filled.reshape(rounds, group_size, local_rows, columns), "data", 1, 1, tiled=True)
    ortho = orthogonalize(owned.reshape(rounds, rows, columns))
    returned = lax.all_to_all(ortho.reshape(rounds, group_size, local_rows, columns), "data", 1, 1, tiled=True)
    mine = returned.reshape(rounds * group_size, local_rows, columns)[:count]
    scale = 0.2 * math.sqrt(max(rows, columns))
    weight_new = weight - LR * (scale * mine.astype(jnp.float32) + WD * weight)
    gathered = lax.all_gather(weight_new.astype(jnp.bfloat16), "data", axis=1, tiled=True)
    return mom_new, weight_new, gathered


def solution(mesh):
    group_size = mesh.shape["data"]
    grad_spec = P(("model", "data"))
    slab_spec = P("model", "data")
    full_spec = P("model")

    def local_step(*arrays):
        results = []
        for family_index in range(4):
            results.extend(family_local(arrays[3 * family_index], arrays[3 * family_index + 1], arrays[3 * family_index + 2], group_size))
        return tuple(results)

    in_specs = (grad_spec, slab_spec, slab_spec) * 4
    out_specs = (slab_spec, slab_spec, full_spec) * 4
    return jax.shard_map(local_step, mesh=mesh, in_specs=in_specs, out_specs=out_specs, check_vma=False)
```

profile of v0, /device:TPU:1, one launch (start us, length us, event | category | flops | bytes accessed | tf_op | source)
XLA Modules:
  0.0 537.9 jit_solution(14148710012476011112)
XLA Ops:
  7.2 10.6 %copy.166 = f32[1,2,896,896]{3,1,2,0:T(2,128)} copy(f32[1,2,896,896]{3,2,1,0:T(8,128)} %param.12) | data formatting | bytes 12845056 | tf_op args[0]
  17.8 2.6 copy.167
  20.5 1.3 copy.102
  21.8 167.8 %all-reduce.11.cloned.1.call-done = (f32[2,896,896]{2,0,1:T(2,128)}, f32[2,896,64]{2,0,1:T(2,128)}, f32[2,896,256]{2,0,1:T(2,128)}, f32[1,256,896]{2,1,0:T(8,128)}) async-done(((f32[2,896,896]{2,0,1:T(2,128)}, f32[2,896,64]{2,0,1:T(2,128)}, f32[2,896,256]{2,0,1:T(2,128)}, f32[1,256,896]{2,1,0:T(8,128)}), (f32[2,896,896]{2,0,1:T(2,128)}, f32[2,896,64]{2,0,1:T(2,128)}, f32[2,896,256]{2,0,1:T(2,128)}, ...) | async-done | bytes 9633808
  189.6 1.3 add_convert_fusion.13
  191.9 6.7 %all-to-all-start.2 = ((bf16[128,2,224]{2,1,0:T(2,128)(2,1)}), bf16[128,2,224]{2,1,0:T(2,128)(2,1)S(1)}, u32[]{:S(2)}, u32[]{:S(2)}) async-start(bf16[128,2,224]{2,1,0:T(2,128)(2,1)} %reshape.710), calls=%async_computation.2 | async-start | bytes 262144 | tf_op jit(solution)/shard_map/all_to_all | solution.py:44
  198.7 1.5 add_convert_fusion.10
  200.4 2.1 copy.97
  202.5 1.4 add_convert_fusion.12
  203.9 1.0 pad_bitcast_fusion.1
  204.9 3.9 all-to-all-done.2
  208.8 6.2 %all-to-all-start = ((bf16[1,128,7,896]{3,2,0,1:T(8,128)(2,1)}), bf16[1,128,7,896]{3,2,0,1:T(8,128)(2,1)S(1)}, u32[]{:S(2)}, u32[]{:S(2)}) async-start(bf16[1,128,7,896]{3,2,0,1:T(8,128)(2,1)} %copy.97), calls=%async_computation | async-start | bytes 3670016 | tf_op jit(solution)/shard_map/all_to_all | solution.py:44
  220.8 24.8 %all-to-all-done = bf16[1,128,7,896]{3,2,0,1:T(8,128)(2,1)S(1)} async-done(((bf16[1,128,7,896]{3,2,0,1:T(8,128)(2,1)}), bf16[1,128,7,896]{3,2,0,1:T(8,128)(2,1)S(1)}, u32[]{:S(2)}, u32[]{:S(2)}) %all-to-all-start) | async-done | bytes 1605664 | tf_op jit(solution)/shard_map/all_to_all | solution.py:44
  245.7 3.8 all-to-all-start.3
  249.5 1.5 fusion
  251.7 1.6 fusion.1
  253.3 2.6 convert_element_type.575
  255.8 3.2 convolution_convert_fusion.4
  259.0 7.7 %add_convert_fusion.8 = bf16[896,896]{1,0:T(8,128)(2,1)} fusion(bf16[896,896]{1,0:T(8,128)(2,1)S(1)} %convert_element_type.575, bf16[896,896]{1,0:T(8,128)(2,1)} %convolution_convert_fusion.4), kind=kOutput, calls=%fused_computation.13 | convolution fusion | flops 2884517888 | bytes 4816896 | tf_op jit(solution)/shard_map/bkj,bjm->bkm/dot_general | solution.py:32
  266.7 5.2 convolution_convert_fusion.3
  271.9 7.7 %add_convert_fusion.6 = bf16[896,896]{1,0:T(8,128)(2,1)} fusion(bf16[896,896]{1,0:T(8,128)(2,1)S(1)} %copy-done.11, bf16[896,896]{1,0:T(8,128)(2,1)} %convolution_convert_fusion.3), kind=kOutput, calls=%fused_computation.11 | convolution fusion | flops 2884517888 | bytes 4816896 | tf_op jit(solution)/shard_map/bkj,bjm->bkm/dot_general | solution.py:32
  279.6 5.2 convolution_convert_fusion.2
  284.8 7.7 %add_convert_fusion.4 = bf16[896,896]{1,0:T(8,128)(2,1)} fusion(bf16[896,896]{1,0:T(8,128)(2,1)S(1)} %copy-done.12, bf16[896,896]{1,0:T(8,128)(2,1)} %convolution_convert_fusion.2), kind=kOutput, calls=%fused_computation.9 | convolution fusion | flops 2884517888 | bytes 4816896 | tf_op jit(solution)/shard_map/bkj,bjm->bkm/dot_general | solution.py:32
  292.5 13.5 %convolution_convert_fusion.1 = bf16[896,896]{1,0:T(8,128)(2,1)} fusion(bf16[896,896]{1,0:T(8,128)(2,1)} %add_convert_fusion.4), kind=kOutput, calls=%fused_computation.17 | convolution fusion | flops 1439449088 | bytes 3211264 | tf_op jit(solution)/shard_map/bkm,bjm->bkj/dot_general | solution.py:29
  306.0 7.3 %add_convert_fusion.2 = bf16[896,896]{1,0:T(8,128)(2,1)S(1)} fusion(bf16[896,896]{1,0:T(8,128)(2,1)} %add_convert_fusion.4, bf16[896,896]{1,0:T(8,128)(2,1)} %convolution_convert_fusion.1), kind=kOutput, calls=%fused_computation.7 | convolution fusion | flops 2884517888 | bytes 4816896 | tf_op jit(solution)/shard_map/bkj,bjm->bkm/dot_general | solution.py:32
  313.3 3.2 convolution_convert_fusion
  316.6 9.9 %all-to-all-start.6 = ((bf16[1,128,2,896]{3,2,0,1:T(2,128)(2,1)}), bf16[1,128,2,896]{3,2,0,1:T(2,128)(2,1)S(1)}, u32[]{:S(2)}, u32[]{:S(2)}) async-start(bf16[1,128,2,896]{3,2,0,1:T(2,128)(2,1)} %pad_bitcast_fusion.1), calls=%async_computation.6 | async-start | bytes 917504 | tf_op jit(solution)/shard_map/all_to_all | solution.py:44
  326.5 7.5 %add_convert_fusion = bf16[896,896]{1,0:T(8,128)(2,1)S(1)} fusion(bf16[896,896]{1,0:T(8,128)(2,1)} %copy-done.10, bf16[896,896]{1,0:T(8,128)(2,1)} %convolution_convert_fusion), kind=kOutput, calls=%fused_computation.5 | convolution fusion | flops 2884517888 | bytes 4816896 | tf_op jit(solution)/shard_map/bkj,bjm->bkm/dot_general | solution.py:32
  333.9 1.5 reshape.697
  335.4 3.7 all-to-all-done.6
  339.2 6.0 %all-to-all-start.1 = ((bf16[1,128,7,896]{3,2,0,1:T(8,128)(2,1)}), bf16[1,128,7,896]{3,2,0,1:T(8,128)(2,1)S(1)}, u32[]{:S(2)}, u32[]{:S(2)}) async-start(bf16[1,128,7,896]{3,2,0,1:T(8,128)(2,1)} %bitcast.2), calls=%async_computation.1 | async-start | bytes 3670016 | tf_op jit(solution)/shard_map/all_to_all | solution.py:46
  345.2 1.3 add_convert_fusion.11
  346.6 1.1 copy.113
  347.9 1.5 fusion.51
  351.0 22.5 %all-to-all-done.1 = bf16[1,128,7,896]{3,2,0,1:T(8,128)(2,1)S(1)} async-done(((bf16[1,128,7,896]{3,2,0,1:T(8,128)(2,1)}), bf16[1,128,7,896]{3,2,0,1:T(8,128)(2,1)S(1)}, u32[]{:S(2)}, u32[]{:S(2)}) %all-to-all-start.1) | async-done | bytes 1605664 | tf_op jit(solution)/shard_map/all_to_all | solution.py:46
  373.5 4.0 all-to-all-start.4
  381.8 0.9 reshape.705
  382.8 8.3 %all-to-all-done.4 = bf16[1,128,7,256]{3,2,0,1:T(8,128)(2,1)S(1)} async-done(((bf16[1,128,7,256]{3,2,0,1:T(8,128)(2,1)}), bf16[1,128,7,256]{3,2,0,1:T(8,128)(2,1)S(1)}, u32[]{:S(2)}, u32[]{:S(2)}) %all-to-all-start.4) | async-done | bytes 458784 | tf_op jit(solution)/shard_map/all_to_all | solution.py:44
  391.1 4.6 all-to-all-start.7
  402.0 0.9 reshape.703
  402.9 5.6 %all-to-all-done.7 = bf16[1,128,2,896]{3,2,0,1:T(2,128)(2,1)S(1)} async-done(((bf16[1,128,2,896]{3,2,0,1:T(2,128)(2,1)}), bf16[1,128,2,896]{3,2,0,1:T(2,128)(2,1)S(1)}, u32[]{:S(2)}, u32[]{:S(2)}) %all-to-all-start.7) | async-done | bytes 458784 | tf_op jit(solution)/shard_map/all_to_all | solution.py:46
  408.5 4.6 all-to-all-start.5
  413.2 39.6 %all_gather.13 = bf16[2,896,64]{2,0,1:T(2,128)(2,1)S(1)} all-gather(bf16[2,7,64]{2,0,1:T(2,128)(2,1)S(1)} %copy.111), channel_id=1, replica_groups=mesh['model'=1,'data'=128] {'data'}, dimensions={1}, use_global_device_ids=true | all-gather | bytes 231168 | tf_op jit(solution)/shard_map/all_gather | solution.py:50
  452.8 1.3 copy.127
  455.3 33.9 %all_gather.15 = bf16[1,256,896]{2,0,1:T(2,128)(2,1)S(1)} all-gather(bf16[1,2,896]{2,0,1:T(2,128)(2,1)S(1)} %copy.123), channel_id=1, replica_groups=mesh['model'=1,'data'=128] {'data'}, dimensions={1}, use_global_device_ids=true | all-gather | bytes 462336 | tf_op jit(solution)/shard_map/all_gather | solution.py:50
  490.1 34.2 %all_gather.14 = bf16[2,896,256]{2,0,1:T(2,128)(2,1)S(1)} all-gather(bf16[2,7,256]{2,0,1:T(2,128)(2,1)S(1)} %copy.120), channel_id=1, replica_groups=mesh['model'=1,'data'=128] {'data'}, dimensions={1}, use_global_device_ids=true | all-gather | bytes 924672 | tf_op jit(solution)/shard_map/all_gather | solution.py:50
  524.3 1.0 copy.129
  526.6 4.0 copy.125
  (98 shorter events, 20.5 us)
Async XLA Ops:
  7.2 10.7 %copy-start = (f32[1,2,896,256]{3,2,1,0:T(8,128)S(1)}, f32[1,2,896,256]{3,2,1,0:T(8,128)}, u32[]{:S(2)}) copy-start(f32[1,2,896,256]{3,2,1,0:T(8,128)} %param.18) | copy-start | bytes 5505028
  7.2 182.4 %all-reduce.11.cloned.1.call-start = ((), (), s32[]{:S(2)}) async-start(), calls=%async_computation.9 | async-start | bytes 20185088
  17.8 2.6 copy-start.1
  21.7 167.8 %copy-start.6 = (f32[2,7,64]{2,0,1:T(2,128)S(1)}, f32[2,7,64]{2,0,1:T(2,128)}, u32[]{:S(2)}) copy-start(f32[2,7,64]{2,0,1:T(2,128)} %param.16) | copy-start | bytes 10756
  21.8 176.9 %copy-start.2 = (f32[2,7,896]{2,0,1:T(2,128)S(1)}, f32[2,7,896]{2,0,1:T(2,128)}, u32[]{:S(2)}) copy-start(f32[2,7,896]{2,0,1:T(2,128)} %param.13) | copy-start | bytes 150532
  191.9 16.8 %all-to-all-start.2 = ((bf16[128,2,224]{2,1,0:T(2,128)(2,1)}), bf16[128,2,224]{2,1,0:T(2,128)(2,1)S(1)}, u32[]{:S(2)}, u32[]{:S(2)}) async-start(bf16[128,2,224]{2,1,0:T(2,128)(2,1)} %reshape.710), calls=%async_computation.2 | async-start | bytes 262144 | tf_op jit(solution)/shard_map/all_to_all | solution.py:44
  200.4 2.2 copy-start.7
  208.8 36.9 %all-to-all-start = ((bf16[1,128,7,896]{3,2,0,1:T(8,128)(2,1)}), bf16[1,128,7,896]{3,2,0,1:T(8,128)(2,1)S(1)}, u32[]{:S(2)}, u32[]{:S(2)}) async-start(bf16[1,128,7,896]{3,2,0,1:T(8,128)(2,1)} %copy.97), calls=%async_computation | async-start | bytes 3670016 | tf_op jit(solution)/shard_map/all_to_all | solution.py:44
  245.7 70.9 %all-to-all-start.3 = ((bf16[128,2,224]{2,1,0:T(2,128)(2,1)}), bf16[128,2,224]{2,1,0:T(2,128)(2,1)S(1)}, u32[]{:S(2)}, u32[]{:S(2)}) async-start(bf16[128,2,224]{2,1,0:T(2,128)(2,1)} %reshape.712), calls=%async_computation.3 | async-start | bytes 262144 | tf_op jit(solution)/shard_map/all_to_all | solution.py:46
  266.7 5.2 copy-start.11
  279.6 5.2 copy-start.12
  313.3 3.2 copy-start.10
  316.6 22.6 %all-to-all-start.6 = ((bf16[1,128,2,896]{3,2,0,1:T(2,128)(2,1)}), bf16[1,128,2,896]{3,2,0,1:T(2,128)(2,1)S(1)}, u32[]{:S(2)}, u32[]{:S(2)}) async-start(bf16[1,128,2,896]{3,2,0,1:T(2,128)(2,1)} %pad_bitcast_fusion.1), calls=%async_computation.6 | async-start | bytes 917504 | tf_op jit(solution)/shard_map/all_to_all | solution.py:44
  339.2 6.0 %copy-start.4 = (f32[2,7,256]{2,0,1:T(2,128)S(1)}, f32[2,7,256]{2,0,1:T(2,128)}, u32[]{:S(2)}) copy-start(f32[2,7,256]{2,0,1:T(2,128)} %param.19) | copy-start | bytes 43012
  339.2 34.3 %all-to-all-start.1 = ((bf16[1,128,7,896]{3,2,0,1:T(8,128)(2,1)}), bf16[1,128,7,896]{3,2,0,1:T(8,128)(2,1)S(1)}, u32[]{:S(2)}, u32[]{:S(2)}) async-start(bf16[1,128,7,896]{3,2,0,1:T(8,128)(2,1)} %bitcast.2), calls=%async_computation.1 | async-start | bytes 3670016 | tf_op jit(solution)/shard_map/all_to_all | solution.py:46
  345.2 2.7 copy-start.8
  350.5 27.1 %copy-start.3 = (f32[2,7,896]{2,0,1:T(2,128)S(1)}, f32[2,7,896]{2,0,1:T(2,128)}, u32[]{:S(2)}) copy-start(f32[2,7,896]{2,0,1:T(2,128)} %param.14) | copy-start | bytes 150532
  373.5 17.6 %all-to-all-start.4 = ((bf16[1,128,7,256]{3,2,0,1:T(8,128)(2,1)}), bf16[1,128,7,256]{3,2,0,1:T(8,128)(2,1)S(1)}, u32[]{:S(2)}, u32[]{:S(2)}) async-start(bf16[1,128,7,256]{3,2,0,1:T(8,128)(2,1)} %copy.113), calls=%async_computation.4 | async-start | bytes 1048576 | tf_op jit(solution)/shard_map/all_to_all | solution.py:44
  377.5 149.1 %all-gather.2.cloned.1.call-start = ((), (), s32[]{:S(2)}) async-start(), calls=%async_computation.8 | async-start | bytes 3236352 | tf_op jit(solution)/shard_map/all_gather | solution.py:50
  391.1 17.5 %all-to-all-start.7 = ((bf16[1,128,2,896]{3,2,0,1:T(2,128)(2,1)}), bf16[1,128,2,896]{3,2,0,1:T(2,128)(2,1)S(1)}, u32[]{:S(2)}, u32[]{:S(2)}) async-start(bf16[1,128,2,896]{3,2,0,1:T(2,128)(2,1)} %bitcast.19), calls=%async_computation.7 | async-start | bytes 917504 | tf_op jit(solution)/shard_map/all_to_all | solution.py:46
  402.0 52.7 %copy-start.9 = (f32[1,2,896]{2,1,0:T(2,128)S(1)}, f32[1,2,896]{2,1,0:T(2,128)}, u32[]{:S(2)}) copy-start(f32[1,2,896]{2,1,0:T(2,128)} %param.23) | copy-start | bytes 21508
  408.5 81.5 %all-to-all-start.5 = ((bf16[1,128,7,256]{3,2,0,1:T(8,128)(2,1)}), bf16[1,128,7,256]{3,2,0,1:T(8,128)(2,1)S(1)}, u32[]{:S(2)}, u32[]{:S(2)}) async-start(bf16[1,128,7,256]{3,2,0,1:T(8,128)(2,1)} %bitcast.14), calls=%async_computation.5 | async-start | bytes 1048576 | tf_op jit(solution)/shard_map/all_to_all | solution.py:46
  452.8 37.3 %copy-start.5 = (f32[2,7,256]{2,0,1:T(2,128)S(1)}, f32[2,7,256]{2,0,1:T(2,128)}, u32[]{:S(2)}) copy-start(f32[2,7,256]{2,0,1:T(2,128)} %param.20) | copy-start | bytes 43012
Sparse Core Ops, SparseCore 0:
  21.9 167.6 all-reduce.10
  381.9 69.6 all-gather.1
where the time goes:
time: 546 us; the launch traced here: 538 us
  waiting for transfers between devices  237 us (43%)
  blocking collectives  108 us (20%)
  matrix products  78.4 us (14%)
  starting transfers between devices  46 us (8%)
  local copies, waits for them, and re-layouts  38.5 us (7%)
  between operations  17.8 us (3%)
  other arithmetic  12.8 us (2%)
    unnamed x3, waiting for transfers between devices  168 us
    all_gather x3, blocking collectives, family_local(): lax.all_gather(weight_new.astype(jnp.bfloat16), 'data', axis=1, tiled=True)  108 us
    dot_general x20, matrix products, orthogonalize(): jnp.einsum(apply_form, poly_mat, ortho, preferred_element_type=jnp.float32)  43.8 us
    all_to_all x4, waiting for transfers between devices, family_local(): lax.all_to_all(filled.reshape(rounds, group_size, local_rows, columns), '...  40.8 us
    dot_general x20, matrix products, orthogonalize(): jnp.einsum(gram_form, ortho, ortho, preferred_element_type=jnp.float32)  34.6 us
    all_to_all x4, waiting for transfers between devices, family_local(): lax.all_to_all(ortho.reshape(rounds, group_size, local_rows, columns), 'd...  28.1 us
    all_to_all x4, starting transfers between devices, family_local(): lax.all_to_all(filled.reshape(rounds, group_size, local_rows, columns), '...  26.9 us
    unnamed x41, local copies, waits for them, and re-layouts  25.8 us
  transfers between devices with their start and end apart: 10, of which 7 were waited for; matrix products, arithmetic and copies ran while one was open for 20% of the time, Pallas kernels for 0%

commit v1 on v0

v1 whole, which is shorter than its diff:
```python
import math
import jax
import jax.numpy as jnp
from jax import lax
from jax.experimental import pallas as pl
from jax.experimental.pallas import tpu as pltpu
from jax.sharding import PartitionSpec as P

NS_STEPS = 5
MU = 0.95
LR = 0.1
WD = 0.5
EPS = 1e-7
COEF_A = 3.4445
COEF_B = -4.7750
COEF_C = 2.0315
GROUP = 128
D = 896
SCALE = 0.2 * math.sqrt(896.0)
MESH = pl.DeviceIdType.MESH
F32 = jnp.float32
BF16 = jnp.bfloat16
DMA = pltpu.SemaphoreType.DMA


def kernel(
    g_sq, g_kv, g_up, g_dn,
    m_sq, m_kv, m_up, m_dn,
    w_sq, w_kv, w_up, w_dn,
    mo_sq, mo_kv, mo_up, mo_dn,
    wo_sq, wo_kv, wo_up, wo_dn,
    b_sq, b_kv, b_up, b_dn,
    br, bp, kvb, upb, dnb, acc,
    r1a, r1b, r1c, r2, r3,
    pieces, recvp, mb, nb, outp, mrecv, outw, wrecv,
    xg, wg, xx, aa, bb, ss, sa, sb,
    vb_sq, vb_kv, vb_up, vb_dn,
    own_s, d2d_s, d2d_r, pre_s, pre_r, mo_s, mo_r, wo_s, wo_r,
    rs1_s, rs1_r, rs2_s, rs2_r, rs3_s, rs3_r,
    u3_s, u3_r, u2_s, u2_r, u1_s, u1_r,
    w3_s, w3_r, w2_s, w2_r, w1_s, w1_r,
    ol_s, or_s, or_r,
):
    me = lax.axis_index("data")
    core = lax.rem(me, 2)
    x = lax.rem(lax.div(me, 2), 4)
    y = lax.rem(lax.div(me, 8), 4)
    z = lax.div(me, 32)
    slot = 2 * x + core
    other = 1 - core
    around = {
        "x": [x] + [lax.rem(x + d, 4) for d in (1, 2, 3)],
        "y": [y] + [lax.rem(y + d, 4) for d in (1, 2, 3)],
        "z": [z] + [lax.rem(z + d, 4) for d in (1, 2, 3)],
    }
    partner = me + other - core
    stride = {"x": 2, "y": 8, "z": 32}
    peers = {dim: [me + (a - around[dim][0]) * stride[dim] for a in around[dim]] for dim in "xyz"}
    row_x = [2 * a - 2 * x for a in around["x"]]

    def peer(dim, delta):
        return peers[dim][delta]

    def remote(src, dst, ssem, rsem, device):
        return pltpu.make_async_remote_copy(
            src_ref=src, dst_ref=dst, send_sem=ssem, recv_sem=rsem,
            device_id={"data": device}, device_id_type=MESH)

    row_peers = [(dx, dc) for dx in range(4) for dc in range(2) if (dx, dc) != (0, 0)]

    row_dev = {(dx, dc): (me, partner)[dc] + row_x[dx] for dx in range(4) for dc in range(2)}
    row_slot = {(dx, dc): 2 * around["x"][dx] + (core, other)[dc] for dx in range(4) for dc in range(2)}

    def row_peer(dx, dc):
        return row_dev[dx, dc]

    barrier = pltpu.get_barrier_semaphore()
    for dx, dc in row_peers:
        pl.semaphore_signal(barrier, inc=1, device_id={"data": row_peer(dx, dc)}, device_id_type=MESH)
    for dim in ("y", "z"):
        for delta in (1, 2, 3):
            pl.semaphore_signal(barrier, inc=1, device_id={"data": peer(dim, delta)}, device_id_type=MESH)

    OFFS = (2, 1, 3, 0)

    def lanes(j):
        return pl.ds(pl.multiple_of(j * 128, 128), 128)

    def common_items(tc, k, w):
        jx, jz = around["x"][OFFS[k]], around["z"][OFFS[k]]
        return [
            (g_sq.at[tc, :, :, :, lanes(jx)], br.at[w, jx]),
            (g_sq.at[tc, jz, :, :, pl.ds(512, 384)], bp.at[w, jz]),
        ]

    def special_items(tc, k, w):
        jz, jy = around["z"][OFFS[k]], around["y"][OFFS[k]]
        if tc == 0:
            return [
                (g_kv.at[0, jz], kvb.at[w, 0, jz]),
                (g_dn.at[:, jy], dnb.at[w, :, jy]),
                (g_kv.at[1, :, jy], kvb.at[w, 1, :, jy]),
            ]
        return [
            (g_up.at[0, jz, :, :, pl.ds(0, 128)], upb.at[w, 0, jz, :, :, pl.ds(0, 128)]),
            (g_up.at[0, :, jy, :, pl.ds(128, 128)], upb.at[w, 0, :, jy, :, pl.ds(128, 128)]),
            (g_up.at[1, :, jy], upb.at[w, 1, :, jy]),
        ]

    def own_copy(k, i, item):
        return pltpu.make_async_copy(item[0], item[1], own_s.at[k, i])

    def par_copy(k, i, item):
        return remote(item[0], item[1], d2d_s.at[k, i], d2d_r.at[k, i], partner)

    def start_own(k):
        for i, item in enumerate(common_items(core, k, 0)):
            own_copy(k, i, item).start()
        for tc in range(2):
            @pl.when(core == tc)
            def _():
                for i, item in enumerate(special_items(tc, k, 0)):
                    own_copy(k, 2 + i, item).start()

    def start_par(k):
        for i, item in enumerate(common_items(other, k, 1)):
            par_copy(k, i, item).start()
        for tc in range(2):
            @pl.when(core == 1 - tc)
            def _():
                for i, item in enumerate(special_items(tc, k, 1)):
                    par_copy(k, 2 + i, item).start()

    def add_chunk(k):
        jx, jy, jz = [around[d][OFFS[k]] for d in "xyz"]
        for i, item in enumerate(common_items(core, k, 0)):
            own_copy(k, i, item).wait()
        for i, item in enumerate(common_items(core, k, 1)):
            par_copy(k, i, item).wait_recv()
        acc[jx] = br[0, jx] + br[1, jx]
        for u in range(3):
            acc[4 + u, jz] = bp[0, jz, :, :, 128 * u:128 * u + 128] + bp[1, jz, :, :, 128 * u:128 * u + 128]

        @pl.when(core == 0)
        def _():
            for i, item in enumerate(special_items(0, k, 0)):
                own_copy(k, 2 + i, item).wait()
            for i, item in enumerate(special_items(0, k, 1)):
                par_copy(k, 2 + i, item).wait_recv()
            acc[7, jz, :, :, 0:64] = kvb[0, 0, jz] + kvb[1, 0, jz]
            acc[7, jz, :, :, 64:128] = jnp.zeros((4, 56, 64), F32)
            rows = dnb[0, :, jy] + dnb[1, :, jy]
            for i in range(7):
                acc[8, :, jy, 8 * i:8 * i + 8, :] = rows[:, 0:8, 128 * i:128 * i + 128]
                acc[9, :, jy, 8 * i:8 * i + 8, :] = rows[:, 8:16, 128 * i:128 * i + 128]
            acc[10, :, jy, :, 0:64] = kvb[0, 1, :, jy] + kvb[1, 1, :, jy]
            acc[10, :, jy, :, 64:128] = jnp.zeros((4, 56, 64), F32)

        @pl.when(core == 1)
        def _():
            for i, item in enumerate(special_items(1, k, 0)):
                own_copy(k, 2 + i, item).wait()
            for i, item in enumerate(special_items(1, k, 1)):
                par_copy(k, 2 + i, item).wait_recv()
            acc[7, jz] = upb[0, 0, jz, :, :, 0:128] + upb[1, 0, jz, :, :, 0:128]
            acc[8, :, jy] = upb[0, 0, :, jy, :, 128:256] + upb[1, 0, :, jy, :, 128:256]
            acc[9, :, jy] = upb[0, 1, :, jy, :, 0:128] + upb[1, 1, :, jy, :, 0:128]
            acc[10, :, jy] = upb[0, 1, :, jy, :, 128:256] + upb[1, 1, :, jy, :, 128:256]

    DIMS1, DIMS2, DIMS3 = ("x", "z", "y"), ("y", "x", "z"), ("z", "y", "x")

    def half1(buf, grp, j, h):
        if grp == 0:
            return buf.at[j, pl.ds(2 * h, 2)]
        if grp == 1:
            return buf.at[pl.ds(4 + 2 * h, 2), j]
        return buf.at[pl.ds(8, 3), pl.ds(2 * h, 2), j]

    def half2(buf, grp, j, h):
        if grp == 0:
            return buf.at[x, pl.ds(2 * h, 2), j]
        if grp == 1:
            return buf.at[4 + j, z, pl.ds(2 * h, 2)]
        return buf.at[pl.ds(8 + 2 * h, 2), j, y]

    def seg3(buf, grp, j):
        if grp == 0:
            return buf.at[x, j, y]
        if grp == 1:
            return buf.at[4 + x, z, j]
        return buf.at[8 + j, z, y]

    def block(buf, grp):
        return buf.at[4 * grp + x, z, y]

    def rs_ring(half, buf, dims, rbufs, ssem, rsem):
        def desc(grp, i):
            dim = dims[grp]
            d, h = ((2, 0), (1, 1), (1, 0), (2, 1), (3, 0), (3, 1))[i]
            src = (around[dim][d], h)
            return remote(half(buf, grp, src[0], src[1]), rbufs[grp].at[i], ssem.at[grp, i], rsem.at[grp, i], peer(dim, 1 if i < 3 else 3))

        def add(grp, j, h, i):
            desc(grp, i).wait_recv()
            ref = half(buf, grp, j, h)
            ref[...] += rbufs[grp][i]

        def first():
            for grp in range(3):
                desc(grp, 0).start()
                desc(grp, 3).start()

        def second():
            for grp in range(3):
                desc(grp, 1).start()
                desc(grp, 4).start()

        def third():
            for grp in range(3):
                p = around[dims[grp]]
                add(grp, p[1], 0, 0)
                desc(grp, 2).start()
                add(grp, p[3], 1, 3)
                desc(grp, 5).start()

        def last():
            for grp in range(3):
                p = around[dims[grp]][0]
                add(grp, p, 1, 1)
                add(grp, p, 0, 4)
            for grp in range(3):
                p = around[dims[grp]][0]
                add(grp, p, 0, 2)
                add(grp, p, 1, 5)

        def drain():
            for grp in range(3):
                for i in range(6):
                    desc(grp, i).wait_send()

        return first, second, third, last, drain

    def ag_ring(half, buf, dims, ssem, rsem):
        def desc(grp, i):
            dim = dims[grp]
            d, h = ((0, 0), (0, 1), (3, 0), (0, 1), (0, 0), (1, 1))[i]
            ref = half(buf, grp, around[dim][d], h)
            return remote(ref, ref, ssem.at[grp, i], rsem.at[grp, i], peer(dim, 1 if i < 3 else 3))

        def first():
            for grp in range(3):
                for i in (0, 3, 1, 4):
                    desc(grp, i).start()

        def second():
            for grp in range(3):
                desc(grp, 0).wait_recv()
                desc(grp, 2).start()
                desc(grp, 3).wait_recv()
                desc(grp, 5).start()

        def last():
            for i in (1, 4, 2, 5):
                for grp in range(3):
                    desc(grp, i).wait_recv()

        def drain():
            for grp in range(3):
                for i in range(6):
                    desc(grp, i).wait_send()

        return first, second, last, drain

    def rs_direct(buf, ssem, rsem):
        def desc(grp, i):
            delta = (2, 1, 3)[i]
            j = around[DIMS3[grp]][delta]
            return remote(seg3(buf, grp, j), r3.at[grp, i], ssem.at[grp, i], rsem.at[grp, i], peer(DIMS3[grp], delta))

        def first():
            for i in range(3):
                for grp in range(3):
                    desc(grp, i).start()

        def last():
            for grp in range(3):
                for i in range(3):
                    desc(grp, i).wait_recv()

        def drain():
            for grp in range(3):
                for i in range(3):
                    desc(grp, i).wait_send()

        return first, last, drain

    def ag_direct(buf, ssem, rsem):
        def desc(grp, i):
            delta = (2, 1, 3)[i]
            ref = block(buf, grp)
            return remote(ref, ref, ssem.at[grp, i], rsem.at[grp, i], peer(DIMS3[grp], delta))

        def first():
            for i in range(3):
                for grp in range(3):
                    desc(grp, i).start()

        def last():
            for grp in range(3):
                for i in range(3):
                    desc(grp, i).wait_recv()

        def drain():
            for grp in range(3):
                for i in range(3):
                    desc(grp, i).wait_send()

        return first, last, drain

    rs1 = rs_ring(half1, acc, DIMS1, (r1a, r1b, r1c), rs1_s, rs1_r)
    rs2 = rs_ring(half2, acc, DIMS2, (r2.at[0], r2.at[1], r2.at[2]), rs2_s, rs2_r)
    rs3 = rs_direct(acc, rs3_s, rs3_r)
    u3 = ag_direct(xg, u3_s, u3_r)
    u2 = ag_ring(half2, xg, DIMS2, u2_s, u2_r)
    u1 = ag_ring(half1, xg, DIMS1, u1_s, u1_r)
    wg3 = ag_direct(wg, w3_s, w3_r)
    wg2 = ag_ring(half2, wg, DIMS2, w2_s, w2_r)
    wg1 = ag_ring(half1, wg, DIMS1, w1_s, w1_r)

    for k in range(4):
        start_own(k)

    for a, (q_sq, q_kv, q_up, q_dn) in enumerate(((m_sq, m_kv, m_up, m_dn), (w_sq, w_kv, w_up, w_dn))):
        for c in range(2):
            for xd in range(4):
                pieces[a, c, xd, 0:7, :] = q_sq[c, :, 128 * xd:128 * xd + 128]
                if xd < 3:
                    pieces[a, c, xd, 8:15, :] = q_sq[c, :, 512 + 128 * xd:640 + 128 * xd]
        pieces[a, 0, 3, 8:15, 0:64] = q_kv[0]
        pieces[a, 0, 2, 16:23, 0:64] = q_kv[1]
        pieces[a, 1, 3, 8:15, :] = q_up[0, :, 0:128]
        pieces[a, 1, 0, 16:23, :] = q_up[0, :, 128:256]
        pieces[a, 1, 1, 16:23, :] = q_up[1, :, 0:128]
        pieces[a, 1, 2, 16:23, :] = q_up[1, :, 128:256]
        for xd in range(2):
            for j in range(7):
                pieces[a, 0, xd, 24 + 2 * j:26 + 2 * j, :] = q_dn[0, :, 128 * j:128 * j + 128]
    acc[11] = jnp.zeros((4, 4, 56, 128), F32)

    pl.semaphore_wait(barrier, 13)

    for k in range(4):
        start_par(k)

    def pre(i):
        dx, dc = row_peers[i]
        return remote(pieces.at[:, (core, other)[dc], around["x"][dx]], recvp.at[slot], pre_s.at[i], pre_r.at[i], row_peer(dx, dc))

    for i in range(7):
        pre(i).start()
    recvp[slot] = pieces[:, core, x]

    add_chunk(0)
    rs1[0]()
    add_chunk(1)
    add_chunk(2)
    rs1[1]()
    add_chunk(3)

    for i in range(7):
        pre(i).wait_recv()
    for a in range(2):
        for g in range(3):
            for s in range(8):
                mb[a, g, 7 * s:7 * s + 7, :] = recvp[s, a, 8 * g:8 * g + 7, :]

    @pl.when(jnp.logical_and(core == 0, x < 2))
    def _():
        for a in range(2):
            for i in range(4):
                for j in range(7):
                    mb[a, 2, 8 * j + 2 * i:8 * j + 2 * i + 2, :] = recvp[4 * x + i, a, 24 + 2 * j:26 + 2 * j, :]

    for g in range(3):
        wg[4 * g + x, z, y] = mb[1, g]

    rs1[2]()
    wg3[0]()
    rs1[3]()
    rs2[0]()
    rs2[1]()
    rs2[2]()
    rs2[3]()
    rs3[0]()
    wg3[1]()
    rs3[1]()

    for g in range(3):
        grad = (acc[4 * g + x, z, y] + r3[g, 0] + r3[g, 1] + r3[g, 2]) * (1.0 / GROUP)
        mom_new = MU * mb[0, g] + grad
        nb[g] = mom_new
        xg[4 * g + x, z, y] = (grad + MU * mom_new).astype(BF16)
    u3[0]()

    def pack_rows(src, dst):
        for s in range(8):
            for g in range(3):
                dst[s, 8 * g:8 * g + 7, :] = src[g, 7 * s:7 * s + 7, :]
            for j in range(7):
                r = 8 * j + 2 * (s % 4)
                dst[s, 24 + 2 * j:26 + 2 * j, :] = src[2, r:r + 2, :]

    def post(src, dst, ssem, rsem, i):
        dx, dc = row_peers[i]
        dest = row_slot[dx, dc]
        return remote(src.at[dest], dst.at[slot], ssem.at[i], rsem.at[i], row_peer(dx, dc))

    def unpack_rows(src, o_sq, o_kv, o_up, o_dn):
        for c in range(2):
            for xs in range(4):
                t = 2 * xs + c
                o_sq[c, :, 128 * xs:128 * xs + 128] = src[t, 0:7, :]
                if xs < 3:
                    o_sq[c, :, 512 + 128 * xs:640 + 128 * xs] = src[t, 8:15, :]
        o_kv[0] = src[6, 8:15, 0:64]
        o_kv[1] = src[4, 16:23, 0:64]
        o_up[0, :, 0:128] = src[7, 8:15, :]
        o_up[0, :, 128:256] = src[1, 16:23, :]
        o_up[1, :, 0:128] = src[3, 16:23, :]
        o_up[1, :, 128:256] = src[5, 16:23, :]
        t = 2 * lax.div(slot, 4)
        for j in range(7):
            o_dn[0, :, 128 * j:128 * j + 128] = src[t, 24 + 2 * j:26 + 2 * j, :]

    pack_rows(nb, outp)
    u3[1]()
    u2[0]()
    u2[1]()
    u2[2]()
    u1[0]()
    for i in range(7):
        post(outp, mrecv, mo_s, mo_r, i).start()
    mrecv[slot] = outp[slot]
    wg2[0]()
    u1[1]()
    wg2[1]()
    u1[2]()

    def total(units, width=128):
        part = jnp.zeros((56, width), F32)
        for u in units:
            v = xg[u].astype(F32)
            part = part + jnp.sum(v * v, axis=(0, 1))[:, 0:width]
        return 1.0 / (jnp.sqrt(jnp.sum(part, keepdims=True)) + EPS)

    def column(u, inv):
        return xg[u].astype(F32).reshape(D, 128) * inv

    inv = total(range(7))
    for u in range(7):
        xx[0, :, 128 * u:128 * u + 128] = column(u, inv).astype(BF16)

    @pl.when(core == 0)
    def _():
        inv_d = total((8, 9))
        both = [(xg[u].astype(F32) * inv_d).reshape(16, 7, 8, 128) for u in (8, 9)]
        both = jnp.concatenate(both, axis=2)
        for j in range(7):
            ss[0, 0, :, 128 * j:128 * j + 128] = both[:, j].reshape(256, 128).astype(BF16)
        inv_0, inv_1 = total((7,), 64), total((10,), 64)
        ss[0, 1, 0:64, :] = column(7, inv_0).T[0:64].astype(BF16)
        ss[0, 1, 64:128, :] = column(10, inv_1).T[0:64].astype(BF16)
        ss[0, 1, 128:256, :] = jnp.zeros((128, D), BF16)

    @pl.when(core == 1)
    def _():
        for i in range(2):
            inv_u = total((7 + 2 * i, 8 + 2 * i))
            for h in range(2):
                ss[0, i, 128 * h:128 * h + 128, :] = column(7 + 2 * i + h, inv_u).T.astype(BF16)

    wg2[2]()
    wg1[0]()

    NT = (((1,), (1,)), ((), ()))
    ROWS = ((0, 256), (256, 256), (512, 256), (768, 128))
    row_id = lax.broadcasted_iota(jnp.int32, (256, 256), 0) // 64
    col_id = lax.broadcasted_iota(jnp.int32, (256, 256), 1) // 64
    keep = jnp.logical_or(row_id == col_id, core == 1)

    def step(it, carry):
        cur = lax.rem(it, 2)
        nxt = 1 - cur
        for r, n in ROWS:
            aa[r:r + n, :] = lax.dot_general(xx[cur, r:r + n, :], xx[cur], NT, preferred_element_type=F32).astype(BF16)
        for i in range(2):
            g = lax.dot_general(ss[cur, i], ss[cur, i], NT, preferred_element_type=F32)
            if i == 1:
                g = jnp.where(keep, g, 0.0)
            sa[i] = g.astype(BF16)

        @pl.when(it == 1)
        def _():
            wg1[1]()

        for r, n in ROWS:
            sq = jnp.dot(aa[r:r + n, :], aa[...], preferred_element_type=F32)
            bb[r:r + n, :] = (COEF_B * aa[r:r + n, :].astype(F32) + COEF_C * sq).astype(BF16)
        for i in range(2):
            sq = jnp.dot(sa[i], sa[i], preferred_element_type=F32)
            sb[i] = (COEF_B * sa[i].astype(F32) + COEF_C * sq).astype(BF16)
        for r, n in ROWS:
            prod = jnp.dot(bb[r:r + n, :], xx[cur], preferred_element_type=F32)
            xx[nxt, r:r + n, :] = (COEF_A * xx[cur, r:r + n, :].astype(F32) + prod).astype(BF16)
        for i in range(2):
            prod = jnp.dot(sb[i], ss[cur, i], preferred_element_type=F32)
            ss[nxt, i] = (COEF_A * ss[cur, i].astype(F32) + prod).astype(BF16)
        return carry

    lax.fori_loop(0, NS_STEPS, step, 0)
    fin = NS_STEPS % 2

    wg1[2]()
    wg1[3]()
    wg2[3]()
    wg3[2]()

    def update(w, v):
        return w - LR * (SCALE * v + WD * w)

    def out_copies(i, refs):
        src, dst = refs
        return (pltpu.make_async_copy(src, dst, ol_s.at[i]),
                remote(src, dst, or_s.at[i], or_r.at[i], partner))

    def sq_refs(p, c):
        return vb_sq.at[pl.ds(112 * p, 112)], b_sq.at[c, pl.ds(112 * p, 112)]

    def small_refs(i, c):
        if c == 0:
            return ((vb_kv.at[0], b_kv.at[0]), (vb_dn, b_dn.at[0]), (vb_kv.at[1], b_kv.at[1]))[i]
        return ((vb_up.at[0], b_up.at[0]), (vb_up.at[1], b_up.at[1]))[i]

    def column_out(u, v, width, dst, lane):
        new = update(wg[u, :, :, :, 0:width].reshape(D, width), v)
        wg[u, :, :, :, 0:width] = new.reshape(4, 4, 56, width)
        dst[:, lane:lane + width] = new.astype(BF16)

    @pl.when(core == 0)
    def _():
        v = ss[fin, 1, 0:128, :].astype(F32).T
        column_out(7, v[:, 0:64], 64, vb_kv.at[0], 0)
        column_out(10, v[:, 64:128], 64, vb_kv.at[1], 0)
        for j in range(7):
            v = ss[fin, 0, :, 128 * j:128 * j + 128].astype(F32).reshape(4, 4, 16, 128)
            lo = update(wg[8, :, :, 8 * j:8 * j + 8, :], v[:, :, 0:8])
            hi = update(wg[9, :, :, 8 * j:8 * j + 8, :], v[:, :, 8:16])
            wg[8, :, :, 8 * j:8 * j + 8, :] = lo
            wg[9, :, :, 8 * j:8 * j + 8, :] = hi
            vb_dn[:, 128 * j:128 * j + 128] = jnp.concatenate([lo, hi], axis=2).reshape(256, 128).astype(BF16)
        for i in range(3):
            for cp in out_copies(8 + i, small_refs(i, 0)):
                cp.start()

    @pl.when(core == 1)
    def _():
        for i in range(2):
            for h in range(2):
                v = ss[fin, i, 128 * h:128 * h + 128, :].astype(F32).T
                column_out(7 + 2 * i + h, v, 128, vb_up.at[i], 128 * h)
        for i in range(2):
            for cp in out_copies(8 + i, small_refs(i, 1)):
                cp.start()

    for p in range(8):
        zz, yy = p // 2, 2 * (p % 2)
        v = xx[fin, 112 * p:112 * p + 112, :].astype(F32)
        for u in range(7):
            new = update(wg[u, zz, yy:yy + 2].reshape(112, 128), v[:, 128 * u:128 * u + 128])
            wg[u, zz, yy:yy + 2] = new.reshape(2, 56, 128)
            vb_sq[112 * p:112 * p + 112, 128 * u:128 * u + 128] = new.astype(BF16)
        for cp in out_copies(p, sq_refs(p, core)):
            cp.start()

    for g in range(3):
        nb[g] = wg[4 * g + x, z, y]
    pack_rows(nb, outw)
    for i in range(7):
        post(outw, wrecv, wo_s, wo_r, i).start()
    wrecv[slot] = outw[slot]

    for i in range(7):
        post(outp, mrecv, mo_s, mo_r, i).wait_recv()
    unpack_rows(mrecv, mo_sq, mo_kv, mo_up, mo_dn)
    for i in range(7):
        post(outw, wrecv, wo_s, wo_r, i).wait_recv()
    unpack_rows(wrecv, wo_sq, wo_kv, wo_up, wo_dn)

    for p in range(8):
        loc, rem = out_copies(p, sq_refs(p, core))
        loc.wait()
        rem.wait()
    for c in range(2):
        @pl.when(core == c)
        def _():
            for i in range(3 - c):
                loc, rem = out_copies(8 + i, small_refs(i, c))
                loc.wait()
                rem.wait_send()
            for i in range(2 + c):
                out_copies(8 + i, small_refs(i, 1 - c))[1].wait_recv()
    for i in range(7):
        pre(i).wait_send()
        post(outp, mrecv, mo_s, mo_r, i).wait_send()
        post(outw, wrecv, wo_s, wo_r, i).wait_send()
    for k in range(4):
        for i, item in enumerate(common_items(other, k, 1)):
            par_copy(k, i, item).wait_send()
        for tc in range(2):
            @pl.when(core == 1 - tc)
            def _():
                for i, item in enumerate(special_items(tc, k, 1)):
                    par_copy(k, 2 + i, item).wait_send()
    rs1[4]()
    rs2[4]()
    rs3[2]()
    u3[2]()
    u2[3]()
    u1[3]()


def solution(mesh):
    grad_spec = P(("model", "data"))
    slab_spec = P("model", "data")
    full_spec = P("model")

    def local_step(g_sq, m_sq, w_sq, g_kv, m_kv, w_kv, g_up, m_up, w_up, g_dn, m_dn, w_dn):
        g_sq = g_sq.reshape(2, 4, 4, 56, 896)
        g_kv = g_kv.reshape(2, 4, 4, 56, 64)
        g_up = g_up.reshape(2, 4, 4, 56, 256)
        g_dn = g_dn.reshape(4, 4, 16, 896)
        vm = pl.BlockSpec(memory_space=pltpu.VMEM)
        hb = pl.BlockSpec(memory_space=pl.ANY)
        rows = [jax.ShapeDtypeStruct(s, F32) for s in ((2, 7, 896), (2, 7, 64), (2, 7, 256), (1, 2, 896))]
        full = [jax.ShapeDtypeStruct(s, BF16) for s in ((2, 896, 896), (2, 896, 64), (2, 896, 256), (1, 256, 896))]
        V = pltpu.VMEM
        scratch = [
            V((2, 4, 4, 4, 56, 128), F32), V((2, 4, 4, 56, 384), F32), V((2, 2, 4, 4, 56, 64), F32),
            V((2, 2, 4, 4, 56, 256), F32), V((2, 4, 4, 16, 896), F32), V((12, 4, 4, 56, 128), F32),
            V((6, 2, 4, 56, 128), F32), V((6, 2, 4, 56, 128), F32), V((6, 3, 2, 56, 128), F32),
            V((3, 6, 2, 56, 128), F32), V((3, 3, 56, 128), F32),
            V((2, 2, 4, 40, 128), F32), V((8, 2, 40, 128), F32), V((2, 3, 56, 128), F32), V((3, 56, 128), F32),
            V((8, 40, 128), F32), V((8, 40, 128), F32), V((8, 40, 128), F32), V((8, 40, 128), F32),
            V((12, 4, 4, 56, 128), BF16), V((12, 4, 4, 56, 128), F32),
            V((2, D, D), BF16), V((D, D), BF16), V((D, D), BF16),
            V((2, 2, 256, D), BF16), V((2, 256, 256), BF16), V((2, 256, 256), BF16),
            V((D, D), BF16), V((2, D, 64), BF16), V((2, D, 256), BF16), V((256, D), BF16),
            DMA((4, 5)), DMA((4, 5)), DMA((4, 5)), DMA((7,)), DMA((7,)), DMA((7,)), DMA((7,)), DMA((7,)), DMA((7,)),
            DMA((3, 6)), DMA((3, 6)), DMA((3, 6)), DMA((3, 6)), DMA((3, 3)), DMA((3, 3)),
            DMA((3, 3)), DMA((3, 3)), DMA((3, 6)), DMA((3, 6)), DMA((3, 6)), DMA((3, 6)),
            DMA((3, 3)), DMA((3, 3)), DMA((3, 6)), DMA((3, 6)), DMA((3, 6)), DMA((3, 6)),
            DMA((11,)), DMA((11,)), DMA((11,)),
        ]
        out = pl.pallas_call(
            kernel,
            out_shape=rows + rows + full,
            in_specs=[hb] * 4 + [vm] * 8,
            out_specs=[vm] * 8 + [hb] * 4,
            scratch_shapes=scratch,
            compiler_params=pltpu.CompilerParams(collective_id=0, has_side_effects=True, vmem_limit_bytes=63_000_000),
            name="muon",
        )(g_sq, g_kv, g_up, g_dn, m_sq, m_kv, m_up, m_dn, w_sq, w_kv, w_up, w_dn)
        m, w, b = out[0:4], out[4:8], out[8:12]
        result = []
        for i in range(4):
            result += [m[i], w[i], b[i]]
        return tuple(result)

    in_specs = (grad_spec, slab_spec, slab_spec) * 4
    out_specs = (slab_spec, slab_spec, full_spec) * 4
    return jax.shard_map(local_step, mesh=mesh, in_specs=in_specs, out_specs=out_specs, check_vma=False)
```

time: 546 us -> 145 us (0.27); the launches traced: 538 us -> 144 us
  waiting for transfers between devices: 237 us -> 0 us
  Pallas kernels: 0 us -> 116 us
  blocking collectives: 108 us -> 0 us
  matrix products: 78.4 us -> 0 us
  starting transfers between devices: 46 us -> 0 us
  between operations: 17.8 us -> 0.67 us
  other arithmetic: 12.8 us -> 0 us
  local copies, waits for them, and re-layouts: 38.5 us -> 27.2 us
    unnamed x3 -> x0, waiting for transfers between devices: 168 us -> none
    pallas_call x0 -> x1, Pallas kernels: none -> 116 us  [local_step(): pl.pallas_call(kernel, out_shape=rows + rows + full, in_specs=[hb] * 4 +...]
    all_gather x3 -> x0, blocking collectives: 108 us -> none  [family_local(): lax.all_gather(weight_new.astype(jnp.bfloat16), 'data', axis=1, tiled=True)]
    dot_general x40 -> x0, matrix products: 78.4 us -> none  [the longest x20 43.8 us: orthogonalize(): jnp.einsum(apply_form, poly_mat, ortho, preferred_element_type=jnp.float32)]
    all_to_all x8 -> x0, waiting for transfers between devices: 68.9 us -> none  [the longest x4 40.8 us: family_local(): lax.all_to_all(filled.reshape(rounds, group_size, local_rows, columns), '...]
    all_to_all x8 -> x0, starting transfers between devices: 45.9 us -> none  [the longest x4 26.9 us: family_local(): lax.all_to_all(filled.reshape(rounds, group_size, local_rows, columns), '...]
    convert_element_type x12 -> x0, other arithmetic: 8.18 us -> none  [the longest x4 5.47 us: family_local(): update = (summed + MU * mom_new).astype(jnp.bfloat16)]
    reshape x11 -> x0, local copies, waits for them, and re-layouts: 8.1 us -> none  [the longest x7 4.62 us: family_local(): filled.reshape(rounds, group_size, local_rows, columns)]
  transfers between devices with their start and end apart: 10 -> 0, of which waited for: 7 -> 0; matrix products, arithmetic and copies ran while one was open for 20% -> 0% of each run, Pallas kernels for 0% -> 0%
where the time goes in v1:
time: 145 us; the launch traced here: 144 us
  Pallas kernels  116 us (80%)
  local copies, waits for them, and re-layouts  27.2 us (19%)
    pallas_call x1, Pallas kernels, local_step(): pl.pallas_call(kernel, out_shape=rows + rows + full, in_specs=[hb] * 4 +...  116 us
    unnamed x27, local copies, waits for them, and re-layouts  27.2 us

profile of v1, /device:TPU:1, one launch (start us, length us, event | category | flops | bytes accessed | tf_op | source)
XLA Modules:
  0.0 144.0 jit_solution(12937487683704766097)
XLA Ops:
  0.6 1.3 copy.26.m_kv
  1.9 1.3 copy.29.w_kv
  3.2 1.3 copy.27.m_up
  4.5 1.3 copy.30.w_up
  5.9 1.4 copy.25.m_sq
  7.3 1.4 copy.28.w_sq
  8.7 2.2 %copy.24 = f32[1,2,896,64]{3,2,1,0:T(8,128)} copy(f32[1,2,896,64]{2,3,1,0:T(8,128)} %param.15) | data formatting | bytes 917504 | tf_op args[3]
  11.0 116.1 %muon.1 = (f32[2,7,896]{2,1,0:T(8,128)}, f32[2,7,64]{2,1,0:T(8,128)}, f32[2,7,256]{2,1,0:T(8,128)}, f32[1,2,896]{2,1,0:T(2,128)}, f32[2,7,896]{2,1,0:T(8,128)}, ...) custom-call(f32[2,4,4,56,896]{4,3,2,1,0:T(8,128)} %bitcast.4, ...), custom_call_target="tpu_custom_call" | custom-call | tf_op jit(solution)/shard_map/muon/pallas_call | solution.py:664
  127.1 1.5 %copy.31 = f32[2,7,896]{2,0,1:T(2,128)} copy(f32[2,7,896]{2,1,0:T(8,128)} %get-tuple-element.36) | data formatting | bytes 100352
  128.6 1.3 copy.33
  129.9 1.3 copy.34
  131.2 1.3 copy.36
  132.5 1.3 copy.37
  133.8 1.5 %copy.32 = f32[2,7,896]{2,0,1:T(2,128)} copy(f32[2,7,896]{2,1,0:T(8,128)} %get-tuple-element.37) | data formatting | bytes 100352
  135.3 1.9 %copy.35 = bf16[2,896,64]{1,2,0:T(8,128)(2,1)} copy(bf16[2,896,64]{2,1,0:T(8,128)(2,1)} %get-tuple-element.41) | data formatting | bytes 458752
  137.2 0.0 copy-start
  137.2 0.0 copy-start.3
  137.2 0.0 copy-start.2
  137.2 0.0 copy-start.1
  137.2 4.0 %copy.43 = bf16[2,896,896]{2,1,0:T(8,128)(2,1)} copy(bf16[2,896,896]{2,1,0:T(8,128)(2,1)} %get-tuple-element.62) | data formatting | bytes 6422528
  141.2 0.0 copy-done
  141.2 0.9 copy.44
  142.1 0.0 copy-done.3
  142.1 0.6 copy.45
  142.7 0.0 copy-done.2
  142.7 0.6 copy.46
  143.3 0.0 copy-done.1
  143.3 0.8 copy.47
Async XLA Ops:
  137.2 4.0 %copy-start = (bf16[2,896,256]{2,1,0:T(8,128)(2,1)S(1)}, bf16[2,896,256]{2,1,0:T(8,128)(2,1)}, u32[]{:S(2)}) copy-start(bf16[2,896,256]{2,1,0:T(8,128)(2,1)} %get-tuple-element.68) | copy-start | bytes 2752516
  137.2 4.9 %copy-start.3 = (f32[1,2,896]{2,1,0:T(2,128)S(1)}, f32[1,2,896]{2,1,0:T(2,128)}, u32[]{:S(2)}) copy-start(f32[1,2,896]{2,1,0:T(2,128)} %get-tuple-element.69) | copy-start | bytes 21508
  137.2 5.5 %copy-start.2 = (f32[1,2,896]{2,1,0:T(2,128)S(1)}, f32[1,2,896]{2,1,0:T(2,128)}, u32[]{:S(2)}) copy-start(f32[1,2,896]{2,1,0:T(2,128)} %get-tuple-element.70) | copy-start | bytes 21508
  137.2 6.1 %copy-start.1 = (bf16[1,256,896]{2,1,0:T(8,128)(2,1)S(1)}, bf16[1,256,896]{2,1,0:T(8,128)(2,1)}, u32[]{:S(2)}) copy-start(bf16[1,256,896]{2,1,0:T(8,128)(2,1)} %get-tuple-element.71) | copy-start | bytes 1376260

commit v2 on v1

v2 whole, which is shorter than its diff:
```python
import math
import jax
import jax.numpy as jnp
from jax import lax
from jax.experimental import pallas as pl
from jax.experimental.pallas import tpu as pltpu
from jax.sharding import PartitionSpec as P

NS_STEPS = 5
MU = 0.95
LR = 0.1
WD = 0.5
EPS = 1e-7
COEF_A = 3.4445
COEF_B = -4.7750
COEF_C = 2.0315
GROUP = 128
D = 896
SCALE = 0.2 * math.sqrt(896.0)
MESH = pl.DeviceIdType.MESH
F32 = jnp.float32
BF16 = jnp.bfloat16
DMA = pltpu.SemaphoreType.DMA


def kernel(
    g_sq, g_kv, g_up, g_dn,
    m_sq, m_kv, m_up, m_dn,
    w_sq, w_kv, w_up, w_dn,
    mrecv, wrecv, vb_sq, vb_kv, vb_up, vb_dn,
    br, bp, kvb, upb, dnb, acc,
    r1a, r1b, r1c, r2, r3,
    q_sq, q_kv, q_up, q_dn,
    pieces, recvp, mb, nb, outp, outw,
    xg, wg, xx, aa, bb, ss, sa, sb,
    own_s, row_s, d2d_s, d2d_r, pre_s, pre_r, mo_s, mo_r, wo_s, wo_r,
    rs1_s, rs1_r, rs2_s, rs2_r, rs3_s, rs3_r,
    u3_s, u3_r, u2_s, u2_r, u1_s, u1_r,
    w3_s, w3_r, w2_s, w2_r, w1_s, w1_r,
    or_s, or_r,
):
    me = lax.axis_index("data")
    core = lax.rem(me, 2)
    x = lax.rem(lax.div(me, 2), 4)
    y = lax.rem(lax.div(me, 8), 4)
    z = lax.div(me, 32)
    slot = 2 * x + core
    other = 1 - core
    around = {
        "x": [x] + [lax.rem(x + d, 4) for d in (1, 2, 3)],
        "y": [y] + [lax.rem(y + d, 4) for d in (1, 2, 3)],
        "z": [z] + [lax.rem(z + d, 4) for d in (1, 2, 3)],
    }
    partner = me + other - core
    stride = {"x": 2, "y": 8, "z": 32}
    peers = {dim: [me + (a - around[dim][0]) * stride[dim] for a in around[dim]] for dim in "xyz"}
    row_x = [2 * a - 2 * x for a in around["x"]]

    def peer(dim, delta):
        return peers[dim][delta]

    def remote(src, dst, ssem, rsem, device):
        return pltpu.make_async_remote_copy(
            src_ref=src, dst_ref=dst, send_sem=ssem, recv_sem=rsem,
            device_id={"data": device}, device_id_type=MESH)

    row_peers = [(dx, dc) for dx in range(4) for dc in range(2) if (dx, dc) != (0, 0)]

    row_dev = {(dx, dc): (me, partner)[dc] + row_x[dx] for dx in range(4) for dc in range(2)}
    row_slot = {(dx, dc): 2 * around["x"][dx] + (core, other)[dc] for dx in range(4) for dc in range(2)}

    def row_peer(dx, dc):
        return row_dev[dx, dc]

    barrier = pltpu.get_barrier_semaphore()
    for dx, dc in row_peers:
        pl.semaphore_signal(barrier, inc=1, device_id={"data": row_peer(dx, dc)}, device_id_type=MESH)
    for dim in ("y", "z"):
        for delta in (1, 2, 3):
            pl.semaphore_signal(barrier, inc=1, device_id={"data": peer(dim, delta)}, device_id_type=MESH)

    OFFS = (2, 1, 3, 0)

    def lanes(j):
        return pl.ds(pl.multiple_of(j * 128, 128), 128)

    def common_items(tc, k, w):
        jx, jz = around["x"][OFFS[k]], around["z"][OFFS[k]]
        return [
            (g_sq.at[tc, :, :, :, lanes(jx)], br.at[w, jx]),
            (g_sq.at[tc, jz, :, :, pl.ds(512, 384)], bp.at[w, jz]),
        ]

    def special_items(tc, k, w):
        jz, jy = around["z"][OFFS[k]], around["y"][OFFS[k]]
        if tc == 0:
            items = [(g_dn.at[:, jy], dnb.at[w, :, jy])]
            return items + [(g_kv, kvb.at[w])] if k == 0 else items
        return [
            (g_up.at[0, jz, :, :, pl.ds(0, 128)], upb.at[w, 0, jz, :, :, pl.ds(0, 128)]),
            (g_up.at[0, :, jy, :, pl.ds(128, 128)], upb.at[w, 0, :, jy, :, pl.ds(128, 128)]),
            (g_up.at[1, :, jy], upb.at[w, 1, :, jy]),
        ]

    def own_copy(k, i, item):
        return pltpu.make_async_copy(item[0], item[1], own_s.at[k, i])

    def par_copy(k, i, item):
        return remote(item[0], item[1], d2d_s.at[k, i], d2d_r.at[k, i], partner)

    def start_own(k):
        for i, item in enumerate(common_items(core, k, 0)):
            own_copy(k, i, item).start()
        for tc in range(2):
            @pl.when(core == tc)
            def _():
                for i, item in enumerate(special_items(tc, k, 0)):
                    own_copy(k, 2 + i, item).start()

    def start_par(k):
        for i, item in enumerate(common_items(other, k, 1)):
            par_copy(k, i, item).start()
        for tc in range(2):
            @pl.when(core == 1 - tc)
            def _():
                for i, item in enumerate(special_items(tc, k, 1)):
                    par_copy(k, 2 + i, item).start()

    def arrive(k, i, own, par):
        own_copy(k, i, own).wait()
        par_copy(k, i, par).wait_recv()

    def add_r(k):
        jx = around["x"][OFFS[k]]
        arrive(k, 0, common_items(core, k, 0)[0], common_items(core, k, 1)[0])
        acc[jx] = br[0, jx] + br[1, jx]

    def add_p(k):
        jz = around["z"][OFFS[k]]
        arrive(k, 1, common_items(core, k, 0)[1], common_items(core, k, 1)[1])
        for u in range(3):
            acc[4 + u, jz] = bp[0, jz, :, :, 128 * u:128 * u + 128] + bp[1, jz, :, :, 128 * u:128 * u + 128]

        @pl.when(core == 1)
        def _():
            arrive(k, 2, special_items(1, k, 0)[0], special_items(1, k, 1)[0])
            acc[7, jz] = upb[0, 0, jz, :, :, 0:128] + upb[1, 0, jz, :, :, 0:128]

    def add_q(k):
        jy = around["y"][OFFS[k]]

        @pl.when(core == 0)
        def _():
            arrive(k, 2, special_items(0, k, 0)[0], special_items(0, k, 1)[0])
            rows = dnb[0, :, jy] + dnb[1, :, jy]
            for i in range(7):
                acc[8, :, jy, 8 * i:8 * i + 8, :] = rows[:, 0:8, 128 * i:128 * i + 128]
                acc[9, :, jy, 8 * i:8 * i + 8, :] = rows[:, 8:16, 128 * i:128 * i + 128]

        @pl.when(core == 1)
        def _():
            for i in (1, 2):
                arrive(k, 2 + i, special_items(1, k, 0)[i], special_items(1, k, 1)[i])
            acc[8, :, jy] = upb[0, 0, :, jy, :, 128:256] + upb[1, 0, :, jy, :, 128:256]
            acc[9, :, jy] = upb[0, 1, :, jy, :, 0:128] + upb[1, 1, :, jy, :, 0:128]
            acc[10, :, jy] = upb[0, 1, :, jy, :, 128:256] + upb[1, 1, :, jy, :, 128:256]

    def add_kv():
        @pl.when(core == 0)
        def _():
            own_copy(0, 3, special_items(0, 0, 0)[1]).wait()
            par_copy(0, 3, special_items(0, 0, 1)[1]).wait_recv()
            acc[7] = (kvb[0] + kvb[1]).reshape(128, D).T.reshape(4, 4, 56, 128)

    DIMS1, DIMS2, DIMS3 = ("x", "z", "y"), ("y", "x", "z"), ("z", "y", "x")

    def half1(buf, grp, j, h):
        if grp == 0:
            return buf.at[j, pl.ds(2 * h, 2)]
        if grp == 1:
            return buf.at[pl.ds(4 + 2 * h, 2), j]
        return buf.at[pl.ds(8, 3), pl.ds(2 * h, 2), j]

    def half2(buf, grp, j, h):
        if grp == 0:
            return buf.at[x, pl.ds(2 * h, 2), j]
        if grp == 1:
            return buf.at[4 + j, z, pl.ds(2 * h, 2)]
        return buf.at[pl.ds(8 + 2 * h, 2), j, y]

    def seg3(buf, grp, j):
        if grp == 0:
            return buf.at[x, j, y]
        if grp == 1:
            return buf.at[4 + x, z, j]
        return buf.at[8 + j, z, y]

    def block(buf, grp):
        return buf.at[4 * grp + x, z, y]

    def rs_ring(half, buf, dims, rbufs, ssem, rsem):
        def desc(grp, i):
            dim = dims[grp]
            d, h = ((2, 0), (1, 1), (1, 0), (2, 1), (3, 0), (3, 1))[i]
            src = (around[dim][d], h)
            return remote(half(buf, grp, src[0], src[1]), rbufs[grp].at[i], ssem.at[grp, i], rsem.at[grp, i], peer(dim, 1 if i < 3 else 3))

        def add(grp, j, h, i):
            desc(grp, i).wait_recv()
            ref = half(buf, grp, j, h)
            ref[...] += rbufs[grp][i]

        def first(groups=(0, 1, 2)):
            for grp in groups:
                desc(grp, 0).start()
                desc(grp, 3).start()

        def second(groups=(0, 1, 2)):
            for grp in groups:
                desc(grp, 1).start()
                desc(grp, 4).start()

        def third(groups=(0, 1, 2)):
            for grp in groups:
                p = around[dims[grp]]
                add(grp, p[1], 0, 0)
                desc(grp, 2).start()
                add(grp, p[3], 1, 3)
                desc(grp, 5).start()

        def last(groups=(0, 1, 2)):
            for grp in groups:
                p = around[dims[grp]][0]
                add(grp, p, 1, 1)
                add(grp, p, 0, 4)
                add(grp, p, 0, 2)
                add(grp, p, 1, 5)

        def drain():
            for grp in range(3):
                for i in range(6):
                    desc(grp, i).wait_send()

        return first, second, third, last, drain

    def ag_ring(half, buf, dims, ssem, rsem):
        def desc(grp, i):
            dim = dims[grp]
            d, h = ((0, 0), (0, 1), (3, 0), (0, 1), (0, 0), (1, 1))[i]
            ref = half(buf, grp, around[dim][d], h)
            return remote(ref, ref, ssem.at[grp, i], rsem.at[grp, i], peer(dim, 1 if i < 3 else 3))

        def first(groups=(0, 1, 2)):
            for grp in groups:
                for i in (0, 3, 1, 4):
                    desc(grp, i).start()

        def second(groups=(0, 1, 2)):
            for grp in groups:
                desc(grp, 0).wait_recv()
                desc(grp, 2).start()
                desc(grp, 3).wait_recv()
                desc(grp, 5).start()

        def last(groups=(0, 1, 2)):
            for grp in groups:
                for i in (1, 4, 2, 5):
                    desc(grp, i).wait_recv()

        def drain():
            for grp in range(3):
                for i in range(6):
                    desc(grp, i).wait_send()

        return first, second, last, drain

    def rs_direct(buf, ssem, rsem):
        def desc(grp, i):
            delta = (2, 1, 3)[i]
            j = around[DIMS3[grp]][delta]
            return remote(seg3(buf, grp, j), r3.at[grp, i], ssem.at[grp, i], rsem.at[grp, i], peer(DIMS3[grp], delta))

        def first(groups=(0, 1, 2)):
            for i in range(3):
                for grp in groups:
                    desc(grp, i).start()

        def last(groups=(0, 1, 2)):
            for grp in groups:
                for i in range(3):
                    desc(grp, i).wait_recv()

        def drain():
            for grp in range(3):
                for i in range(3):
                    desc(grp, i).wait_send()

        return first, last, drain

    def ag_direct(buf, ssem, rsem):
        def desc(grp, i):
            delta = (2, 1, 3)[i]
            ref = block(buf, grp)
            return remote(ref, ref, ssem.at[grp, i], rsem.at[grp, i], peer(DIMS3[grp], delta))

        def first(groups=(0, 1, 2)):
            for i in range(3):
                for grp in groups:
                    desc(grp, i).start()

        def last(groups=(0, 1, 2)):
            for grp in groups:
                for i in range(3):
                    desc(grp, i).wait_recv()

        def drain():
            for grp in range(3):
                for i in range(3):
                    desc(grp, i).wait_send()

        return first, last, drain

    rs1 = rs_ring(half1, acc, DIMS1, (r1a, r1b, r1c), rs1_s, rs1_r)
    rs2 = rs_ring(half2, acc, DIMS2, (r2.at[0], r2.at[1], r2.at[2]), rs2_s, rs2_r)
    rs3 = rs_direct(acc, rs3_s, rs3_r)
    u3 = ag_direct(xg, u3_s, u3_r)
    u2 = ag_ring(half2, xg, DIMS2, u2_s, u2_r)
    u1 = ag_ring(half1, xg, DIMS1, u1_s, u1_r)
    wg3 = ag_direct(wg, w3_s, w3_r)
    wg2 = ag_ring(half2, wg, DIMS2, w2_s, w2_r)
    wg1 = ag_ring(half1, wg, DIMS1, w1_s, w1_r)

    for k in range(4):
        start_own(k)

    def row_copies():
        pairs = ((m_sq, w_sq, q_sq), (m_kv, w_kv, q_kv), (m_up, w_up, q_up), (m_dn, w_dn, q_dn))
        return [pltpu.make_async_copy(src[a], src[2].at[a], row_s.at[a, i]) for i, src in enumerate(pairs) for a in range(2)]

    for cp in row_copies():
        cp.start()

    def pack_pieces():
        for cp in row_copies():
            cp.wait()
        for a in range(2):
            for c in range(2):
                for xd in range(4):
                    pieces[a, c, xd, 0:7, :] = q_sq[a, :, c, 128 * xd:128 * xd + 128]
                    if xd < 3:
                        pieces[a, c, xd, 8:15, :] = q_sq[a, :, c, 512 + 128 * xd:640 + 128 * xd]
            pieces[a, 0, 3, 8:15, 0:64] = q_kv[a, :, 0, :]
            pieces[a, 0, 3, 8:15, 64:128] = q_kv[a, :, 1, :]
            pieces[a, 1, 3, 8:15, :] = q_up[a, :, 0, 0:128]
            pieces[a, 1, 0, 16:23, :] = q_up[a, :, 0, 128:256]
            pieces[a, 1, 1, 16:23, :] = q_up[a, :, 1, 0:128]
            pieces[a, 1, 2, 16:23, :] = q_up[a, :, 1, 128:256]
            for xd in range(2):
                for j in range(7):
                    pieces[a, 0, xd, 24 + 2 * j:26 + 2 * j, :] = q_dn[a, 0, :, 128 * j:128 * j + 128]

    acc[11] = jnp.zeros((4, 4, 56, 128), F32)

    @pl.when(core == 0)
    def _():
        acc[10] = jnp.zeros((4, 4, 56, 128), F32)

    pack_pieces()
    pl.semaphore_wait(barrier, 13)

    for k in range(4):
        start_par(k)

    def pre(a, i):
        dx, dc = row_peers[i]
        return remote(pieces.at[a, (core, other)[dc], around["x"][dx]], recvp.at[a, slot], pre_s.at[a, i], pre_r.at[a, i], row_peer(dx, dc))

    def pre_start(a):
        for i in range(7):
            pre(a, i).start()
        recvp[a, slot] = pieces[a, core, x]

    def pre_done(a):
        for i in range(7):
            pre(a, i).wait_recv()
        for g in range(3):
            for s in range(8):
                mb[a, g, 7 * s:7 * s + 7, :] = recvp[a, s, 8 * g:8 * g + 7, :]

        @pl.when(jnp.logical_and(core == 0, x < 2))
        def _():
            for i in range(4):
                for j in range(7):
                    mb[a, 2, 8 * j + 2 * i:8 * j + 2 * i + 2, :] = recvp[a, 4 * x + i, 24 + 2 * j:26 + 2 * j, :]

    pre_start(0)
    add_r(0)
    rs1[0]((0,))
    add_q(0)
    rs1[0]((2,))
    add_p(0)
    add_kv()
    rs1[0]((1,))
    for add, g in ((add_r, 0), (add_p, 1), (add_q, 2)):
        add(1)
        add(2)
        rs1[1]((g,))
    for add in (add_r, add_p, add_q):
        add(3)
    pre_done(0)

    ORDER = (2, 1, 0)
    for g in ORDER:
        rs1[2]((g,))
    for g in ORDER:
        rs1[3]((g,))
        rs2[0]((g,))
        rs2[1]((g,))
    for g in ORDER:
        rs2[2]((g,))
    for g in ORDER:
        rs2[3]((g,))
        rs3[0]((g,))
    pre_start(1)
    for g in ORDER:
        rs3[1]((g,))
        grad = (acc[4 * g + x, z, y] + r3[g, 0] + r3[g, 1] + r3[g, 2]) * (1.0 / GROUP)
        mom_new = MU * mb[0, g] + grad
        nb[g] = mom_new
        xg[4 * g + x, z, y] = (grad + MU * mom_new).astype(BF16)
        u3[0]((g,))

    def pack_rows(src, dst):
        for s in range(8):
            for g in range(3):
                dst[s, 8 * g:8 * g + 7, :] = src[g, 7 * s:7 * s + 7, :]
            for j in range(7):
                r = 8 * j + 2 * (s % 4)
                dst[s, 24 + 2 * j:26 + 2 * j, :] = src[2, r:r + 2, :]

    def post(src, dst, ssem, rsem, i):
        dx, dc = row_peers[i]
        dest = row_slot[dx, dc]
        return remote(src.at[dest], dst.at[slot], ssem.at[i], rsem.at[i], row_peer(dx, dc))

    pack_rows(nb, outp)
    pre_done(1)
    for g in range(3):
        wg[4 * g + x, z, y] = mb[1, g]
    for g in ORDER:
        u3[1]((g,))
        u2[0]((g,))
    for g in ORDER:
        u2[1]((g,))
    wg3[0]()
    for g in ORDER:
        u2[2]((g,))
        u1[0]((g,))
    for g in ORDER:
        u1[1]((g,))
    for i in range(7):
        post(outp, mrecv, mo_s, mo_r, i).start()
    mrecv[slot] = outp[slot]
    wg3[1]()
    wg2[0]()
    for g in ORDER:
        u1[2]((g,))

    def total(units):
        part = jnp.zeros((56, 128), F32)
        for u in units:
            v = xg[u].astype(F32)
            part = part + jnp.sum(v * v, axis=(0, 1))
        return 1.0 / (jnp.sqrt(jnp.sum(part, keepdims=True)) + EPS)

    def column(u, inv):
        return xg[u].astype(F32).reshape(D, 128) * inv

    inv = total(range(7))
    for u in range(7):
        xx[0, :, 128 * u:128 * u + 128] = column(u, inv).astype(BF16)

    @pl.when(core == 0)
    def _():
        inv_d = total((8, 9))
        both = [(xg[u].astype(F32) * inv_d).reshape(16, 7, 8, 128) for u in (8, 9)]
        both = jnp.concatenate(both, axis=2)
        for j in range(7):
            ss[0, 0, :, 128 * j:128 * j + 128] = both[:, j].reshape(256, 128).astype(BF16)
        v = xg[7].astype(F32)
        v = v.reshape(D, 128).T
        for i in range(2):
            h = v[64 * i:64 * i + 64]
            norm = jnp.sqrt(jnp.sum(h * h, keepdims=True))
            ss[0, 1, 64 * i:64 * i + 64, :] = (h * (1.0 / (norm + EPS))).astype(BF16)
        ss[0, 1, 128:256, :] = jnp.zeros((128, D), BF16)

    @pl.when(core == 1)
    def _():
        for i in range(2):
            inv_u = total((7 + 2 * i, 8 + 2 * i))
            for h in range(2):
                ss[0, i, 128 * h:128 * h + 128, :] = column(7 + 2 * i + h, inv_u).T.astype(BF16)

    wg2[1]()

    NT = (((1,), (1,)), ((), ()))
    ROWS = ((0, 256), (256, 256), (512, 256), (768, 128))
    row_id = lax.broadcasted_iota(jnp.int32, (256, 256), 0) // 64
    col_id = lax.broadcasted_iota(jnp.int32, (256, 256), 1) // 64
    keep = jnp.logical_or(row_id == col_id, core == 1)

    def symmetric(product, out):
        for r in (0, 256, 512):
            value = product(r, 256, r, 768 - r)
            out[r:r + 256, r:768] = value
            if r < 512:
                out[r + 256:768, r:r + 256] = value[:, 256:].T
        value = product(768, 128, 0, D)
        out[768:896, :] = value
        out[0:768, 768:896] = value[:, 0:768].T

    def step(it, carry):
        cur = lax.rem(it, 2)
        nxt = 1 - cur
        def gram(r, n, c, m):
            return lax.dot_general(xx[cur, r:r + n, :], xx[cur, c:c + m, :], NT, preferred_element_type=F32).astype(BF16)

        symmetric(gram, aa)
        for i in range(2):
            g = lax.dot_general(ss[cur, i], ss[cur, i], NT, preferred_element_type=F32)
            if i == 1:
                g = jnp.where(keep, g, 0.0)
            sa[i] = g.astype(BF16)

        @pl.when(it == 0)
        def _():
            wg2[2]()
            wg1[0]()

        @pl.when(it == 2)
        def _():
            wg1[1]()

        def poly(r, n, c, m):
            sq = jnp.dot(aa[r:r + n, :], aa[:, c:c + m], preferred_element_type=F32)
            return (COEF_B * aa[r:r + n, c:c + m].astype(F32) + COEF_C * sq).astype(BF16)

        symmetric(poly, bb)
        for i in range(2):
            sq = jnp.dot(sa[i], sa[i], preferred_element_type=F32)
            sb[i] = (COEF_B * sa[i].astype(F32) + COEF_C * sq).astype(BF16)
        for r, n in ROWS:
            prod = jnp.dot(bb[r:r + n, :], xx[cur], preferred_element_type=F32)
            xx[nxt, r:r + n, :] = (COEF_A * xx[cur, r:r + n, :].astype(F32) + prod).astype(BF16)
        for i in range(2):
            prod = jnp.dot(sb[i], ss[cur, i], preferred_element_type=F32)
            ss[nxt, i] = (COEF_A * ss[cur, i].astype(F32) + prod).astype(BF16)
        return carry

    lax.fori_loop(0, NS_STEPS, step, 0)
    fin = NS_STEPS % 2

    wg1[2]()
    wg1[3]()
    wg2[3]()
    wg3[2]()

    def update(w, v):
        return w - LR * (SCALE * v + WD * w)

    def out_copy(i, ref):
        return remote(ref, ref, or_s.at[i], or_r.at[i], partner)

    def sq_ref(p, c):
        return vb_sq.at[c, pl.ds(112 * p, 112)]

    def small_refs(c):
        return (vb_kv, vb_dn) if c == 0 else (vb_up.at[0], vb_up.at[1])

    def column_new(u, v):
        new = update(wg[u].reshape(D, 128), v)
        wg[u] = new.reshape(4, 4, 56, 128)
        return new

    @pl.when(core == 0)
    def _():
        v = ss[fin, 1, 0:128, :].astype(F32).T
        vb_kv[...] = column_new(7, v).T.astype(BF16)
        for j in range(7):
            v = ss[fin, 0, :, 128 * j:128 * j + 128].astype(F32).reshape(4, 4, 16, 128)
            lo = update(wg[8, :, :, 8 * j:8 * j + 8, :], v[:, :, 0:8])
            hi = update(wg[9, :, :, 8 * j:8 * j + 8, :], v[:, :, 8:16])
            wg[8, :, :, 8 * j:8 * j + 8, :] = lo
            wg[9, :, :, 8 * j:8 * j + 8, :] = hi
            vb_dn[:, 128 * j:128 * j + 128] = jnp.concatenate([lo, hi], axis=2).reshape(256, 128).astype(BF16)
        for i in range(2):
            out_copy(8 + i, small_refs(0)[i]).start()

    @pl.when(core == 1)
    def _():
        for i in range(2):
            for h in range(2):
                v = ss[fin, i, 128 * h:128 * h + 128, :].astype(F32).T
                vb_up[i, :, 128 * h:128 * h + 128] = column_new(7 + 2 * i + h, v).astype(BF16)
        for i in range(2):
            out_copy(8 + i, small_refs(1)[i]).start()

    for p in range(8):
        zz, yy = p // 2, 2 * (p % 2)
        v = xx[fin, 112 * p:112 * p + 112, :].astype(F32)
        for u in range(7):
            new = update(wg[u, zz, yy:yy + 2].reshape(112, 128), v[:, 128 * u:128 * u + 128])
            wg[u, zz, yy:yy + 2] = new.reshape(2, 56, 128)
            vb_sq[core, 112 * p:112 * p + 112, 128 * u:128 * u + 128] = new.astype(BF16)
        out_copy(p, sq_ref(p, core)).start()

    for g in range(3):
        nb[g] = wg[4 * g + x, z, y]
    pack_rows(nb, outw)
    for i in range(7):
        post(outw, wrecv, wo_s, wo_r, i).start()
    wrecv[slot] = outw[slot]

    for i in range(7):
        post(outp, mrecv, mo_s, mo_r, i).wait_recv()
        post(outw, wrecv, wo_s, wo_r, i).wait_recv()

    for p in range(8):
        out_copy(p, sq_ref(p, core)).wait()
    for c in range(2):
        @pl.when(core == c)
        def _():
            for i in range(2):
                out_copy(8 + i, small_refs(c)[i]).wait_send()
                out_copy(8 + i, small_refs(1 - c)[i]).wait_recv()
    for i in range(7):
        pre(0, i).wait_send()
        pre(1, i).wait_send()
        post(outp, mrecv, mo_s, mo_r, i).wait_send()
        post(outw, wrecv, wo_s, wo_r, i).wait_send()
    for k in range(4):
        for i, item in enumerate(common_items(other, k, 1)):
            par_copy(k, i, item).wait_send()
        for tc in range(2):
            @pl.when(core == 1 - tc)
            def _():
                for i, item in enumerate(special_items(tc, k, 1)):
                    par_copy(k, 2 + i, item).wait_send()
    rs1[4]()
    rs2[4]()
    rs3[2]()
    u3[2]()
    u2[3]()
    u1[3]()


def unpack_rows(slot, src, o_sq, o_kv, o_up, o_dn):
    for c in range(2):
        for xs in range(4):
            t = 2 * xs + c
            o_sq[:, c, 128 * xs:128 * xs + 128] = src[t, 0:7, :]
            if xs < 3:
                o_sq[:, c, 512 + 128 * xs:640 + 128 * xs] = src[t, 8:15, :]
    o_kv[:, 0, :] = src[6, 8:15, 0:64]
    o_kv[:, 1, :] = src[6, 8:15, 64:128]
    o_up[:, 0, 0:128] = src[7, 8:15, :]
    o_up[:, 0, 128:256] = src[1, 16:23, :]
    o_up[:, 1, 0:128] = src[3, 16:23, :]
    o_up[:, 1, 128:256] = src[5, 16:23, :]
    t = 2 * lax.div(slot, 4)
    for j in range(7):
        o_dn[0, :, 128 * j:128 * j + 128] = src[t, 24 + 2 * j:26 + 2 * j, :]


def write_out(
    mrecv, wrecv, vb_sq, vb_kv, vb_up, vb_dn,
    mo_sq, mo_kv, mo_up, mo_dn, wo_sq, wo_kv, wo_up, wo_dn, b_sq, b_kv, b_up, b_dn, sem,
):
    copies = [pltpu.make_async_copy(src, dst, sem.at[i]) for i, (src, dst) in enumerate(
        ((vb_sq, b_sq), (vb_kv, b_kv), (vb_up, b_up), (vb_dn, b_dn)))]
    for cp in copies:
        cp.start()
    me = lax.axis_index("data")
    slot = lax.rem(me, 8)
    unpack_rows(slot, mrecv, mo_sq, mo_kv, mo_up, mo_dn)
    unpack_rows(slot, wrecv, wo_sq, wo_kv, wo_up, wo_dn)
    for cp in copies:
        cp.wait()


def solution(mesh):
    grad_spec = P(("model", "data"))
    slab_spec = P("model", "data")
    full_spec = P("model")

    def local_step(g_sq, m_sq, w_sq, g_kv, m_kv, w_kv, g_up, m_up, w_up, g_dn, m_dn, w_dn):
        g_sq = g_sq.reshape(2, 4, 4, 56, 896)
        g_kv = g_kv[0].transpose(0, 2, 1)
        g_up = g_up.reshape(2, 4, 4, 56, 256)
        g_dn = g_dn.reshape(4, 4, 16, 896)
        vm = pl.BlockSpec(memory_space=pltpu.VMEM)
        hb = pl.BlockSpec(memory_space=pltpu.HBM)
        V = pltpu.VMEM
        scratch = [
            V((2, 4, 4, 4, 56, 128), F32), V((2, 4, 4, 56, 384), F32), V((2, 2, 64, 896), F32),
            V((2, 2, 4, 4, 56, 256), F32), V((2, 4, 4, 16, 896), F32), V((12, 4, 4, 56, 128), F32),
            V((6, 2, 4, 56, 128), F32), V((6, 2, 4, 56, 128), F32), V((6, 3, 2, 56, 128), F32),
            V((3, 6, 2, 56, 128), F32), V((3, 3, 56, 128), F32),
            V((2, 7, 2, 896), F32), V((2, 7, 2, 64), F32), V((2, 7, 2, 256), F32), V((2, 1, 2, 896), F32),
            V((2, 2, 4, 40, 128), F32), V((2, 8, 40, 128), F32), V((2, 3, 56, 128), F32), V((3, 56, 128), F32),
            V((8, 40, 128), F32), V((8, 40, 128), F32),
            V((12, 4, 4, 56, 128), BF16), V((12, 4, 4, 56, 128), F32),
            V((2, D, D), BF16), V((D, D), BF16), V((D, D), BF16),
            V((2, 2, 256, D), BF16), V((2, 256, 256), BF16), V((2, 256, 256), BF16),
            DMA((4, 5)), DMA((2, 4)), DMA((4, 5)), DMA((4, 5)), DMA((2, 7)), DMA((2, 7)), DMA((7,)), DMA((7,)), DMA((7,)), DMA((7,)),
            DMA((3, 6)), DMA((3, 6)), DMA((3, 6)), DMA((3, 6)), DMA((3, 3)), DMA((3, 3)),
            DMA((3, 3)), DMA((3, 3)), DMA((3, 6)), DMA((3, 6)), DMA((3, 6)), DMA((3, 6)),
            DMA((3, 3)), DMA((3, 3)), DMA((3, 6)), DMA((3, 6)), DMA((3, 6)), DMA((3, 6)),
            DMA((10,)), DMA((10,)),
        ]

        def rows(a):
            return a.transpose(1, 0, 2)

        mid = [V(s, F32) for s in ((8, 40, 128), (8, 40, 128))]
        mid += [V(s, BF16) for s in ((2, D, D), (128, D), (2, D, 256), (256, D))]
        parts = pl.pallas_call(
            kernel,
            out_shape=mid,
            in_specs=[hb] * 12,
            out_specs=[vm] * 6,
            scratch_shapes=scratch,
            compiler_params=pltpu.CompilerParams(collective_id=0, has_side_effects=True, vmem_limit_bytes=61700000),
            name="muon",
        )(g_sq, g_kv, g_up, g_dn, rows(m_sq), rows(m_kv), rows(m_up), m_dn, rows(w_sq), rows(w_kv), rows(w_up), w_dn)
        small = [jax.ShapeDtypeStruct(s, F32) for s in ((7, 2, 896), (7, 2, 64), (7, 2, 256), (1, 2, 896))]
        full = [jax.ShapeDtypeStruct(s, BF16) for s in ((2, D, D), (128, D), (2, D, 256), (256, D))]
        out = pl.pallas_call(
            write_out,
            out_shape=small + small + full,
            in_specs=[vm] * 6,
            out_specs=[vm] * 8 + [hb] * 4,
            scratch_shapes=[DMA((4,))],
            compiler_params=pltpu.CompilerParams(vmem_limit_bytes=4_000_000),
            name="write_out",
        )(*parts)
        m, w, b = out[0:4], out[4:8], out[8:12]
        return (
            rows(m[0]), rows(w[0]), b[0],
            rows(m[1]), rows(w[1]), b[1].reshape(2, 64, D).transpose(0, 2, 1),
            rows(m[2]), rows(w[2]), b[2],
            m[3], w[3], b[3].reshape(1, 256, D),
        )

    in_specs = (grad_spec, slab_spec, slab_spec) * 4
    out_specs = (slab_spec, slab_spec, full_spec) * 4
    return jax.shard_map(local_step, mesh=mesh, in_specs=in_specs, out_specs=out_specs, check_vma=False)
```

time: 145 us -> 112 us (0.77)
  local copies, waits for them, and re-layouts: 27.2 us -> 0 us
  Pallas kernels: 116 us -> 111 us
    unnamed x27 -> x0, local copies, waits for them, and re-layouts: 27.2 us -> none
    pallas_call x1 -> x2, Pallas kernels: 116 us -> 111 us  [the longest x1 109 us: local_step(): pl.pallas_call(kernel, out_shape=mid, in_specs=[hb] * 12, out_specs=[vm]...]
where the time goes in v2:
time: 112 us
  Pallas kernels  111 us (99%)
    pallas_call x1, Pallas kernels, local_step(): pl.pallas_call(kernel, out_shape=mid, in_specs=[hb] * 12, out_specs=[vm]...  109 us
    pallas_call x1, Pallas kernels, local_step(): pl.pallas_call(write_out, out_shape=small + small + full, in_specs=[vm] *...  2.91 us

profile of v2, /device:TPU:1, one launch (start us, length us, event | category | flops | bytes accessed | tf_op | source)
XLA Modules:
  0.0 112.1 jit_solution(4184198759363740711)
XLA Ops:
  0.6 108.5 %muon.1 = (f32[8,40,128]{2,1,0:T(8,128)S(1)}, f32[8,40,128]{2,1,0:T(8,128)S(1)}, bf16[2,896,896]{2,1,0:T(8,128)(2,1)S(1)}, bf16[128,896]{1,0:T(8,128)(2,1)S(1)},...) custom-call(f32[2,4,4,56,896]{4,3,2,1,0:T(8,128)} %bitcast.22, f32[2,64,896]{2,1,0:T(8,128)} %bitcast.25, ...), custom_call_target="tpu_custom_call" | custom-call | tf_op jit(solution)/shard_map/muon/pallas_call | solution.py:728
  109.2 2.9 %write_out.1 = (f32[7,2,896]{2,1,0:T(2,128)}, f32[7,2,64]{2,1,0:T(2,128)}, f32[7,2,256]{2,1,0:T(2,128)}, f32[1,2,896]{2,1,0:T(2,128)}, f32[7,2,896]{2,1,0:T(2,12...) custom-call(f32[8,40,128]{2,1,0:T(8,128)S(1)} %get-tuple-element.30., ...), custom_call_target="tpu_custom_call" | custom-call | tf_op jit(solution)/shard_map/write_out/pallas_call | solution.py:739

commit v3 on v2

--- a/solution.py
+++ b/solution.py
@@ -29,13 +29,13 @@
     w_sq, w_kv, w_up, w_dn,
     mrecv, wrecv, vb_sq, vb_kv, vb_up, vb_dn,
     br, bp, kvb, upb, dnb, acc,
-    r1a, r1b, r1c, r2, r3,
+    r1a, r1b, r1c, r2, r3, s3, mg, mt,
     q_sq, q_kv, q_up, q_dn,
     pieces, recvp, mb, nb, outp, outw,
     xg, wg, xx, aa, bb, ss, sa, sb,
     own_s, row_s, d2d_s, d2d_r, pre_s, pre_r, mo_s, mo_r, wo_s, wo_r,
     rs1_s, rs1_r, rs2_s, rs2_r, rs3_s, rs3_r,
-    u3_s, u3_r, u2_s, u2_r, u1_s, u1_r,
+    m3_s, m3_r, u2_s, u2_r, u1_s, u1_r,
     w3_s, w3_r, w2_s, w2_r, w1_s, w1_r,
     or_s, or_r,
 ):
@@ -188,12 +188,12 @@
             return buf.at[4 + j, z, pl.ds(2 * h, 2)]
         return buf.at[pl.ds(8 + 2 * h, 2), j, y]
 
-    def seg3(buf, grp, j):
+    def half3(buf, grp, h):
         if grp == 0:
-            return buf.at[x, j, y]
+            return buf.at[x, pl.ds(2 * h, 2), y]
         if grp == 1:
-            return buf.at[4 + x, z, j]
-        return buf.at[8 + j, z, y]
+            return buf.at[4 + x, z, pl.ds(2 * h, 2)]
+        return buf.at[pl.ds(8 + 2 * h, 2), z, y]
 
     def block(buf, grp):
         return buf.at[4 * grp + x, z, y]
@@ -274,28 +274,38 @@
 
         return first, second, last, drain
 
-    def rs_direct(buf, ssem, rsem):
-        def desc(grp, i):
-            delta = (2, 1, 3)[i]
-            j = around[DIMS3[grp]][delta]
-            return remote(seg3(buf, grp, j), r3.at[grp, i], ssem.at[grp, i], rsem.at[grp, i], peer(DIMS3[grp], delta))
+    swap = {}
+    for d in "xyz":
+        p = around[d][0]
+        swap[d] = (me + (1 - 2 * lax.rem(p, 2)) * stride[d], me + (3 - 2 * p) * stride[d])
+
+    def sum_pairs():
+        def desc(grp, st, h):
+            src = half3(acc, grp, h) if st == 0 else s3.at[grp, h]
+            return remote(src, r3.at[grp, st, h], rs3_s.at[grp, 2 * st + h], rs3_r.at[grp, 2 * st + h], swap[DIMS3[grp]][(st + h) % 2])
 
         def first(groups=(0, 1, 2)):
-            for i in range(3):
-                for grp in groups:
-                    desc(grp, i).start()
-
-        def last(groups=(0, 1, 2)):
-            for grp in groups:
-                for i in range(3):
-                    desc(grp, i).wait_recv()
+            for grp in groups:
+                for h in range(2):
+                    desc(grp, 0, h).start()
+
+        def second(groups=(0, 1, 2)):
+            for grp in groups:
+                for h in range(2):
+                    desc(grp, 0, h).wait_recv()
+                    s3[grp, h] = half3(acc, grp, h)[...] + r3[grp, 0, h]
+                    desc(grp, 1, h).start()
+
+        def last(grp, h):
+            desc(grp, 1, h).wait_recv()
+            return s3[grp, h] + r3[grp, 1, h]
 
         def drain():
             for grp in range(3):
-                for i in range(3):
-                    desc(grp, i).wait_send()
-
-        return first, last, drain
+                for i in range(4):
+                    desc(grp, i // 2, i % 2).wait_send()
+
+        return first, second, last, drain
 
     def ag_direct(buf, ssem, rsem):
         def desc(grp, i):
@@ -322,8 +332,8 @@
 
     rs1 = rs_ring(half1, acc, DIMS1, (r1a, r1b, r1c), rs1_s, rs1_r)
     rs2 = rs_ring(half2, acc, DIMS2, (r2.at[0], r2.at[1], r2.at[2]), rs2_s, rs2_r)
-    rs3 = rs_direct(acc, rs3_s, rs3_r)
-    u3 = ag_direct(xg, u3_s, u3_r)
+    rs3 = sum_pairs()
+    m3 = ag_direct(mg, m3_s, m3_r)
     u2 = ag_ring(half2, xg, DIMS2, u2_s, u2_r)
     u1 = ag_ring(half1, xg, DIMS1, u1_s, u1_r)
     wg3 = ag_direct(wg, w3_s, w3_r)
@@ -418,17 +428,25 @@
         rs2[1]((g,))
     for g in ORDER:
         rs2[2]((g,))
+    for g in range(3):
+        mg[4 * g + x, z, y] = mb[0, g]
+    m3[0]()
     for g in ORDER:
         rs2[3]((g,))
         rs3[0]((g,))
     pre_start(1)
     for g in ORDER:
         rs3[1]((g,))
-        grad = (acc[4 * g + x, z, y] + r3[g, 0] + r3[g, 1] + r3[g, 2]) * (1.0 / GROUP)
-        mom_new = MU * mb[0, g] + grad
-        nb[g] = mom_new
-        xg[4 * g + x, z, y] = (grad + MU * mom_new).astype(BF16)
-        u3[0]((g,))
+    m3[1]()
+    for g in ORDER:
+        for h in range(2):
+            grad = rs3[2](g, h) * (1.0 / GROUP)
+            mom_new = MU * half3(mg, g, h)[...] + grad
+            mt[g, 2 * h:2 * h + 2] = mom_new
+            half3(xg, g, h)[...] = (grad + MU * mom_new).astype(BF16)
+        u2[0]((g,))
+    for g in range(3):
+        nb[g] = mt[g, around[DIMS3[g]][0]]
 
     def pack_rows(src, dst):
         for s in range(8):
@@ -443,19 +461,16 @@
         dest = row_slot[dx, dc]
         return remote(src.at[dest], dst.at[slot], ssem.at[i], rsem.at[i], row_peer(dx, dc))
 
-    pack_rows(nb, outp)
+    for g in ORDER:
+        u2[1]((g,))
     pre_done(1)
     for g in range(3):
         wg[4 * g + x, z, y] = mb[1, g]
-    for g in ORDER:
-        u3[1]((g,))
-        u2[0]((g,))
-    for g in ORDER:
-        u2[1]((g,))
     wg3[0]()
     for g in ORDER:
         u2[2]((g,))
         u1[0]((g,))
+    pack_rows(nb, outp)
     for g in ORDER:
         u1[1]((g,))
     for i in range(7):
@@ -520,9 +535,7 @@
         out[768:896, :] = value
         out[0:768, 768:896] = value[:, 0:768].T
 
-    def step(it, carry):
-        cur = lax.rem(it, 2)
-        nxt = 1 - cur
+    def poly_step(cur, it):
         def gram(r, n, c, m):
             return lax.dot_general(xx[cur, r:r + n, :], xx[cur, c:c + m, :], NT, preferred_element_type=F32).astype(BF16)
 
@@ -533,13 +546,10 @@
                 g = jnp.where(keep, g, 0.0)
             sa[i] = g.astype(BF16)
 
-        @pl.when(it == 0)
-        def _():
+        if it == 0:
             wg2[2]()
             wg1[0]()
-
-        @pl.when(it == 2)
-        def _():
+        if it == 2:
             wg1[1]()
 
         def poly(r, n, c, m):
@@ -550,16 +560,31 @@
         for i in range(2):
             sq = jnp.dot(sa[i], sa[i], preferred_element_type=F32)
             sb[i] = (COEF_B * sa[i].astype(F32) + COEF_C * sq).astype(BF16)
-        for r, n in ROWS:
-            prod = jnp.dot(bb[r:r + n, :], xx[cur], preferred_element_type=F32)
-            xx[nxt, r:r + n, :] = (COEF_A * xx[cur, r:r + n, :].astype(F32) + prod).astype(BF16)
+
+    def apply_small(cur, nxt):
         for i in range(2):
             prod = jnp.dot(sb[i], ss[cur, i], preferred_element_type=F32)
             ss[nxt, i] = (COEF_A * ss[cur, i].astype(F32) + prod).astype(BF16)
+
+    def apply_rows(cur, r, n):
+        prod = jnp.dot(bb[pl.ds(r, n), :], xx[cur], preferred_element_type=F32)
+        return (COEF_A * xx[cur, pl.ds(r, n), :].astype(F32) + prod).astype(BF16)
+
+    def step(it, carry):
+        cur = it % 2
+        nxt = 1 - cur
+        poly_step(cur, it)
+        for r, n in ROWS:
+            xx[nxt, r:r + n, :] = apply_rows(cur, r, n)
+        apply_small(cur, nxt)
         return carry
 
-    lax.fori_loop(0, NS_STEPS, step, 0)
-    fin = NS_STEPS % 2
+    for it in range(NS_STEPS - 1):
+        step(it, 0)
+    cur = (NS_STEPS - 1) % 2
+    fin = 1 - cur
+    poly_step(cur, None)
+    apply_small(cur, fin)
 
     wg1[2]()
     wg1[3]()
@@ -573,7 +598,7 @@
         return remote(ref, ref, or_s.at[i], or_r.at[i], partner)
 
     def sq_ref(p, c):
-        return vb_sq.at[c, pl.ds(112 * p, 112)]
+        return vb_sq.at[c, pl.ds(pl.multiple_of(224 * p, 32), 224)]
 
     def small_refs(c):
         return (vb_kv, vb_dn) if c == 0 else (vb_up.at[0], vb_up.at[1])
@@ -606,28 +631,28 @@
         for i in range(2):
             out_copy(8 + i, small_refs(1)[i]).start()
 
-    for p in range(8):
-        zz, yy = p // 2, 2 * (p % 2)
-        v = xx[fin, 112 * p:112 * p + 112, :].astype(F32)
+    for i in range(4):
+        q = around["z"][i]
+        v = apply_rows(cur, pl.multiple_of(224 * q, 32), 224).astype(F32)
         for u in range(7):
-            new = update(wg[u, zz, yy:yy + 2].reshape(112, 128), v[:, 128 * u:128 * u + 128])
-            wg[u, zz, yy:yy + 2] = new.reshape(2, 56, 128)
-            vb_sq[core, 112 * p:112 * p + 112, 128 * u:128 * u + 128] = new.astype(BF16)
-        out_copy(p, sq_ref(p, core)).start()
-
-    for g in range(3):
-        nb[g] = wg[4 * g + x, z, y]
-    pack_rows(nb, outw)
-    for i in range(7):
-        post(outw, wrecv, wo_s, wo_r, i).start()
-    wrecv[slot] = outw[slot]
+            new = update(wg[u, q].reshape(224, 128), v[:, 128 * u:128 * u + 128])
+            wg[u, q] = new.reshape(4, 56, 128)
+            vb_sq[core, pl.ds(pl.multiple_of(224 * q, 32), 224), 128 * u:128 * u + 128] = new.astype(BF16)
+        out_copy(i, sq_ref(q, core)).start()
+        if i == 0:
+            for g in range(3):
+                nb[g] = wg[4 * g + x, z, y]
+            pack_rows(nb, outw)
+            for k in range(7):
+                post(outw, wrecv, wo_s, wo_r, k).start()
+            wrecv[slot] = outw[slot]
 
     for i in range(7):
         post(outp, mrecv, mo_s, mo_r, i).wait_recv()
         post(outw, wrecv, wo_s, wo_r, i).wait_recv()
 
-    for p in range(8):
-        out_copy(p, sq_ref(p, core)).wait()
+    for p in range(4):
+        out_copy(p, sq_ref(around["z"][p], core)).wait()
     for c in range(2):
         @pl.when(core == c)
         def _():
@@ -649,8 +674,8 @@
                     par_copy(k, 2 + i, item).wait_send()
     rs1[4]()
     rs2[4]()
-    rs3[2]()
-    u3[2]()
+    rs3[3]()
+    m3[2]()
     u2[3]()
     u1[3]()
 
@@ -706,7 +731,8 @@
             V((2, 4, 4, 4, 56, 128), F32), V((2, 4, 4, 56, 384), F32), V((2, 2, 64, 896), F32),
             V((2, 2, 4, 4, 56, 256), F32), V((2, 4, 4, 16, 896), F32), V((12, 4, 4, 56, 128), F32),
             V((6, 2, 4, 56, 128), F32), V((6, 2, 4, 56, 128), F32), V((6, 3, 2, 56, 128), F32),
-            V((3, 6, 2, 56, 128), F32), V((3, 3, 56, 128), F32),
+            V((3, 6, 2, 56, 128), F32), V((3, 2, 2, 2, 56, 128), F32), V((3, 2, 2, 56, 128), F32),
+            V((12, 4, 4, 56, 128), F32), V((3, 4, 56, 128), F32),
             V((2, 7, 2, 896), F32), V((2, 7, 2, 64), F32), V((2, 7, 2, 256), F32), V((2, 1, 2, 896), F32),
             V((2, 2, 4, 40, 128), F32), V((2, 8, 40, 128), F32), V((2, 3, 56, 128), F32), V((3, 56, 128), F32),
             V((8, 40, 128), F32), V((8, 40, 128), F32),
@@ -714,7 +740,7 @@
             V((2, D, D), BF16), V((D, D), BF16), V((D, D), BF16),
             V((2, 2, 256, D), BF16), V((2, 256, 256), BF16), V((2, 256, 256), BF16),
             DMA((4, 5)), DMA((2, 4)), DMA((4, 5)), DMA((4, 5)), DMA((2, 7)), DMA((2, 7)), DMA((7,)), DMA((7,)), DMA((7,)), DMA((7,)),
-            DMA((3, 6)), DMA((3, 6)), DMA((3, 6)), DMA((3, 6)), DMA((3, 3)), DMA((3, 3)),
+            DMA((3, 6)), DMA((3, 6)), DMA((3, 6)), DMA((3, 6)), DMA((3, 4)), DMA((3, 4)),
             DMA((3, 3)), DMA((3, 3)), DMA((3, 6)), DMA((3, 6)), DMA((3, 6)), DMA((3, 6)),
             DMA((3, 3)), DMA((3, 3)), DMA((3, 6)), DMA((3, 6)), DMA((3, 6)), DMA((3, 6)),
             DMA((10,)), DMA((10,)),

time: 112 us -> 103 us (0.920)
  Pallas kernels: 111 us -> 102 us
    pallas_call x1, Pallas kernels: 109 us -> 99.6 us  [local_step(): pl.pallas_call(kernel, out_shape=mid, in_specs=[hb] * 12, out_specs=[vm]...]
where the time goes in v3:
time: 103 us
  Pallas kernels  102 us (99%)
    pallas_call x1, Pallas kernels, local_step(): pl.pallas_call(kernel, out_shape=mid, in_specs=[hb] * 12, out_specs=[vm]...  99.6 us
    pallas_call x1, Pallas kernels, local_step(): pl.pallas_call(write_out, out_shape=small + small + full, in_specs=[vm] *...  2.91 us

profile of v3, /device:TPU:1, one launch (start us, length us, event | category | flops | bytes accessed | tf_op | source)
XLA Modules:
  0.0 103.3 jit_solution(6567337787657127210)
XLA Ops:
  0.6 99.6 %muon.1 = (f32[8,40,128]{2,1,0:T(8,128)S(1)}, f32[8,40,128]{2,1,0:T(8,128)S(1)}, bf16[2,896,896]{2,1,0:T(8,128)(2,1)S(1)}, bf16[128,896]{1,0:T(8,128)(2,1)S(1)},...) custom-call(f32[2,4,4,56,896]{4,3,2,1,0:T(8,128)} %bitcast.22, f32[2,64,896]{2,1,0:T(8,128)} %bitcast.25, ...), custom_call_target="tpu_custom_call" | custom-call | tf_op jit(solution)/shard_map/muon/pallas_call | solution.py:754
  100.2 2.9 %write_out.1 = (f32[7,2,896]{2,1,0:T(2,128)}, f32[7,2,64]{2,1,0:T(2,128)}, f32[7,2,256]{2,1,0:T(2,128)}, f32[1,2,896]{2,1,0:T(2,128)}, f32[7,2,896]{2,1,0:T(2,12...) custom-call(f32[8,40,128]{2,1,0:T(8,128)S(1)} %get-tuple-element.30., ...), custom_call_target="tpu_custom_call" | custom-call | tf_op jit(solution)/shard_map/write_out/pallas_call | solution.py:765

commit v4 on v3

v4 whole, which is shorter than its diff:
```python
import math
import jax
import jax.numpy as jnp
from jax import lax
from jax.experimental import pallas as pl
from jax.experimental.pallas import tpu as pltpu
from jax.sharding import PartitionSpec as P

NS_STEPS = 5
MU = 0.95
LR = 0.1
WD = 0.5
EPS = 1e-7
COEF_A = 3.4445
COEF_B = -4.7750
COEF_C = 2.0315
GROUP = 128
D = 896
SCALE = 0.2 * math.sqrt(896.0)
GROUPS = 3
PAIR = 2
ALL = tuple(range(GROUPS))
RING = 4
HOPS = 6
SLAB = 7
SUB = 8
UNITS = 12
PEERS = 13
P_END = 15
TILE16 = 16
Q_END = 23
DOWN_AT = 24
DOWN_NEXT = 26
ALIGN = 32
PACK = 40
BROWS = 56
KVD = 64
LANES = 128
QROWS = 224
FF = 256
TRIO = 384
HALF_D = 512
P_AT = 640
TAIL_D = 768
PACKED = (SUB, PACK, LANES)
MESH = pl.DeviceIdType.MESH
F32 = jnp.float32
BF16 = jnp.bfloat16
DMA = pltpu.SemaphoreType.DMA


def kernel(
    g_sq, g_kv, g_up, g_dn,
    m_sq, m_kv, m_up, m_dn,
    w_sq, w_kv, w_up, w_dn,
    mrecv, wrecv, vb_sq, vb_kv, vb_up, vb_dn,
    br, bp, kvb, upb, dnb, acc,
    r1a, r1b, r1c, r2, r3, s3, mg, mt,
    q_sq, q_kv, q_up, q_dn,
    pieces, recvp, mb, nb, outp, outw,
    xg, wg, xx, aa, bb, ss, sa, sb,
    own_s, row_s, d2d_s, d2d_r, pre_s, pre_r, mo_s, mo_r, wo_s, wo_r,
    rs1_s, rs1_r, rs2_s, rs2_r, rs3_s, rs3_r,
    m3_s, m3_r, u2_s, u2_r, u1_s, u1_r,
    w3_s, w3_r, w2_s, w2_r, w1_s, w1_r,
    or_s, or_r,
):
    me = lax.axis_index("data")
    core = lax.rem(me, 2)
    x = lax.rem(lax.div(me, 2), RING)
    y = lax.rem(lax.div(me, SUB), RING)
    z = lax.div(me, ALIGN)
    slot = 2 * x + core
    other = 1 - core
    around = {
        "x": [x] + [lax.rem(x + d, RING) for d in (1, 2, 3)],
        "y": [y] + [lax.rem(y + d, RING) for d in (1, 2, 3)],
        "z": [z] + [lax.rem(z + d, RING) for d in (1, 2, 3)],
    }
    partner = me + other - core
    stride = {"x": 2, "y": SUB, "z": ALIGN}
    peers = {dim: [me + (a - around[dim][0]) * stride[dim] for a in around[dim]] for dim in "xyz"}
    row_x = [2 * a - 2 * x for a in around["x"]]

    def peer(dim, delta):
        return peers[dim][delta]

    def remote(src, dst, ssem, rsem, device):
        return pltpu.make_async_remote_copy(
            src_ref=src, dst_ref=dst, send_sem=ssem, recv_sem=rsem,
            device_id={"data": device}, device_id_type=MESH)

    row_peers = [(dx, dc) for dx in range(RING) for dc in range(PAIR) if (dx, dc) != (0, 0)]

    row_dev = {(dx, dc): (me, partner)[dc] + row_x[dx] for dx in range(RING) for dc in range(PAIR)}
    row_slot = {(dx, dc): 2 * around["x"][dx] + (core, other)[dc] for dx in range(RING) for dc in range(PAIR)}

    def row_peer(dx, dc):
        return row_dev[dx, dc]

    barrier = pltpu.get_barrier_semaphore()
    for dx, dc in row_peers:
        pl.semaphore_signal(barrier, inc=1, device_id={"data": row_peer(dx, dc)}, device_id_type=MESH)
    for dim in ("y", "z"):
        for delta in (1, 2, 3):
            pl.semaphore_signal(barrier, inc=1, device_id={"data": peer(dim, delta)}, device_id_type=MESH)

    OFFS = (2, 1, 3, 0)

    def lanes(j):
        return pl.ds(pl.multiple_of(j * LANES, LANES), LANES)

    def common_items(tc, k, w):
        jx, jz = around["x"][OFFS[k]], around["z"][OFFS[k]]
        return [
            (g_sq.at[tc, :, :, :, lanes(jx)], br.at[w, jx]),
            (g_sq.at[tc, jz, :, :, pl.ds(HALF_D, TRIO)], bp.at[w, jz]),
        ]

    def special_items(tc, k, w):
        jz, jy = around["z"][OFFS[k]], around["y"][OFFS[k]]
        if tc == 0:
            items = [(g_dn.at[:, jy], dnb.at[w, :, jy])]
            return items + [(g_kv, kvb.at[w])] if k == 0 else items
        return [
            (g_up.at[0, jz, :, :, pl.ds(0, LANES)], upb.at[w, 0, jz, :, :, pl.ds(0, LANES)]),
            (g_up.at[0, :, jy, :, pl.ds(LANES, LANES)], upb.at[w, 0, :, jy, :, pl.ds(LANES, LANES)]),
            (g_up.at[1, :, jy], upb.at[w, 1, :, jy]),
        ]

    def own_copy(k, i, item):
        return pltpu.make_async_copy(item[0], item[1], own_s.at[k, i])

    def par_copy(k, i, item):
        return remote(item[0], item[1], d2d_s.at[k, i], d2d_r.at[k, i], partner)

    def start_own(k):
        for i, item in enumerate(common_items(core, k, 0)):
            own_copy(k, i, item).start()
        for tc in range(PAIR):
            @pl.when(core == tc)
            def _():
                for i, item in enumerate(special_items(tc, k, 0)):
                    own_copy(k, 2 + i, item).start()

    def start_par(k):
        for i, item in enumerate(common_items(other, k, 1)):
            par_copy(k, i, item).start()
        for tc in range(PAIR):
            @pl.when(core == 1 - tc)
            def _():
                for i, item in enumerate(special_items(tc, k, 1)):
                    par_copy(k, 2 + i, item).start()

    def common(k, w):
        return common_items(core, k, w)

    def down_kv(k, w):
        return special_items(0, k, w)

    def ups(k, w):
        return special_items(1, k, w)

    def arrive(k, i, items, at):
        own_copy(k, i, items(k, 0)[at]).wait()
        par_copy(k, i, items(k, 1)[at]).wait_recv()

    def add_r(k):
        jx = around["x"][OFFS[k]]
        arrive(k, 0, common, 0)
        acc[jx] = br[0, jx] + br[1, jx]

    def add_p(k):
        jz = around["z"][OFFS[k]]
        arrive(k, 1, common, 1)
        for u in range(GROUPS):
            acc[RING + u, jz] = bp[0, jz, :, :, LANES * u:LANES * u + LANES] + bp[1, jz, :, :, LANES * u:LANES * u + LANES]

        @pl.when(core == 1)
        def _():
            arrive(k, PAIR, ups, 0)
            acc[SLAB, jz] = upb[0, 0, jz, :, :, :LANES] + upb[1, 0, jz, :, :, :LANES]

    def add_q(k):
        jy = around["y"][OFFS[k]]

        @pl.when(core == 0)
        def _():
            arrive(k, PAIR, down_kv, 0)
            rows = dnb[0, :, jy] + dnb[1, :, jy]
            for i in range(SLAB):
                acc[SUB, :, jy, SUB * i:SUB * i + SUB, :] = rows[:, :SUB, LANES * i:LANES * i + LANES]
                acc[9, :, jy, SUB * i:SUB * i + SUB, :] = rows[:, SUB:TILE16, LANES * i:LANES * i + LANES]

        @pl.when(core == 1)
        def _():
            for i in (1, 2):
                arrive(k, PAIR + i, ups, i)
            acc[SUB, :, jy] = upb[0, 0, :, jy, :, LANES:FF] + upb[1, 0, :, jy, :, LANES:FF]
            acc[9, :, jy] = upb[0, 1, :, jy, :, :LANES] + upb[1, 1, :, jy, :, :LANES]
            acc[10, :, jy] = upb[0, 1, :, jy, :, LANES:FF] + upb[1, 1, :, jy, :, LANES:FF]

    def add_kv():
        @pl.when(core == 0)
        def _():
            arrive(0, GROUPS, down_kv, 1)
            acc[SLAB] = (kvb[0] + kvb[1]).reshape(LANES, D).T.reshape(RING, RING, BROWS, LANES)

    DIMS1, DIMS2, DIMS3 = ("x", "z", "y"), ("y", "x", "z"), ("z", "y", "x")

    def half1(buf, grp, j, h):
        if grp == 0:
            return buf.at[j, pl.ds(PAIR * h, PAIR)]
        if grp == 1:
            return buf.at[pl.ds(RING + PAIR * h, PAIR), j]
        return buf.at[pl.ds(SUB, 3), pl.ds(PAIR * h, PAIR), j]

    def half2(buf, grp, j, h):
        if grp == 0:
            return buf.at[x, pl.ds(PAIR * h, PAIR), j]
        if grp == 1:
            return buf.at[RING + j, z, pl.ds(PAIR * h, PAIR)]
        return buf.at[pl.ds(SUB + PAIR * h, PAIR), j, y]

    def half3(buf, grp, h):
        if grp == 0:
            return buf.at[x, pl.ds(PAIR * h, PAIR), y]
        if grp == 1:
            return buf.at[RING + x, z, pl.ds(PAIR * h, PAIR)]
        return buf.at[pl.ds(SUB + PAIR * h, PAIR), z, y]

    def block(buf, grp):
        return buf.at[RING * grp + x, z, y]

    def rs_ring(half, buf, dims, rbufs, ssem, rsem):
        def desc(grp, i):
            dim = dims[grp]
            d, h = ((2, 0), (1, 1), (1, 0), (2, 1), (3, 0), (3, 1))[i]
            src = (around[dim][d], h)
            return remote(half(buf, grp, src[0], src[1]), rbufs[grp].at[i], ssem.at[grp, i], rsem.at[grp, i], peer(dim, 1 if i < GROUPS else GROUPS))

        def add(grp, j, h, i):
            desc(grp, i).wait_recv()
            ref = half(buf, grp, j, h)
            ref[...] += rbufs[grp][i]

        def first(groups=ALL):
            for grp in groups:
                desc(grp, 0).start()
                desc(grp, 3).start()

        def second(groups=ALL):
            for grp in groups:
                desc(grp, 1).start()
                desc(grp, RING).start()

        def third(groups=ALL):
            for grp in groups:
                p = around[dims[grp]]
                add(grp, p[1], 0, 0)
                desc(grp, 2).start()
                add(grp, p[3], 1, 3)
                desc(grp, 5).start()

        def last(groups=ALL):
            for grp in groups:
                p = around[dims[grp]][0]
                add(grp, p, 1, 1)
                add(grp, p, 0, RING)
                add(grp, p, 0, 2)
                add(grp, p, 1, 5)

        def drain():
            for grp in range(GROUPS):
                for i in range(HOPS):
                    desc(grp, i).wait_send()

        return first, second, third, last, drain

    def ag_ring(half, buf, dims, ssem, rsem):
        def desc(grp, i):
            dim = dims[grp]
            d, h = ((0, 0), (0, 1), (3, 0), (0, 1), (0, 0), (1, 1))[i]
            ref = half(buf, grp, around[dim][d], h)
            return remote(ref, ref, ssem.at[grp, i], rsem.at[grp, i], peer(dim, 1 if i < GROUPS else GROUPS))

        def first(groups=ALL):
            for grp in groups:
                for i in (0, 3, 1, RING):
                    desc(grp, i).start()

        def second(groups=ALL):
            for grp in groups:
                desc(grp, 0).wait_recv()
                desc(grp, 2).start()
                desc(grp, 3).wait_recv()
                desc(grp, 5).start()

        def last(groups=ALL):
            for grp in groups:
                for i in (1, RING, 2, 5):
                    desc(grp, i).wait_recv()

        def drain():
            for grp in range(GROUPS):
                for i in range(HOPS):
                    desc(grp, i).wait_send()

        return first, second, last, drain

    swap = {}
    for d in "xyz":
        p = around[d][0]
        swap[d] = (me + (1 - 2 * lax.rem(p, 2)) * stride[d], me + (3 - 2 * p) * stride[d])

    def sum_pairs():
        def desc(grp, st, h):
            src = half3(acc, grp, h) if st == 0 else s3.at[grp, h]
            return remote(src, r3.at[grp, st, h], rs3_s.at[grp, 2 * st + h], rs3_r.at[grp, 2 * st + h], swap[DIMS3[grp]][(st + h) % 2])

        def first(groups=ALL):
            for grp in groups:
                for h in range(PAIR):
                    desc(grp, 0, h).start()

        def second(groups=ALL):
            for grp in groups:
                for h in range(PAIR):
                    desc(grp, 0, h).wait_recv()
                    s3[grp, h] = half3(acc, grp, h)[...] + r3[grp, 0, h]
                    desc(grp, 1, h).start()

        def last(grp, h):
            desc(grp, 1, h).wait_recv()
            return s3[grp, h] + r3[grp, 1, h]

        def drain():
            for grp in range(GROUPS):
                for i in range(RING):
                    desc(grp, i // 2, i % 2).wait_send()

        return first, second, last, drain

    def ag_direct(buf, ssem, rsem):
        def desc(grp, i):
            delta = (2, 1, 3)[i]
            ref = block(buf, grp)
            return remote(ref, ref, ssem.at[grp, i], rsem.at[grp, i], peer(DIMS3[grp], delta))

        def first(groups=ALL):
            for i in range(GROUPS):
                for grp in groups:
                    desc(grp, i).start()

        def last(groups=ALL):
            for grp in groups:
                for i in range(GROUPS):
                    desc(grp, i).wait_recv()

        def drain():
            for grp in range(GROUPS):
                for i in range(GROUPS):
                    desc(grp, i).wait_send()

        return first, last, drain

    rs1 = rs_ring(half1, acc, DIMS1, (r1a, r1b, r1c), rs1_s, rs1_r)
    rs2 = rs_ring(half2, acc, DIMS2, (r2.at[0], r2.at[1], r2.at[2]), rs2_s, rs2_r)
    rs3 = sum_pairs()
    m3 = ag_direct(mg, m3_s, m3_r)
    u2 = ag_ring(half2, xg, DIMS2, u2_s, u2_r)
    u1 = ag_ring(half1, xg, DIMS1, u1_s, u1_r)
    wg3 = ag_direct(wg, w3_s, w3_r)
    wg2 = ag_ring(half2, wg, DIMS2, w2_s, w2_r)
    wg1 = ag_ring(half1, wg, DIMS1, w1_s, w1_r)

    for k in range(RING):
        start_own(k)

    def row_copies():
        pairs = ((m_sq, w_sq, q_sq), (m_kv, w_kv, q_kv), (m_up, w_up, q_up), (m_dn, w_dn, q_dn))
        return [pltpu.make_async_copy(src[a], src[2].at[a], row_s.at[a, i]) for i, src in enumerate(pairs) for a in range(PAIR)]

    for cp in row_copies():
        cp.start()

    def pack_pieces():
        for cp in row_copies():
            cp.wait()
        for a in range(PAIR):
            for c in range(PAIR):
                for xd in range(RING):
                    pieces[a, c, xd, :SLAB, :] = q_sq[a, :, c, LANES * xd:LANES * xd + LANES]
                    if xd < 3:
                        pieces[a, c, xd, SUB:P_END, :] = q_sq[a, :, c, HALF_D + LANES * xd:P_AT + LANES * xd]
            pieces[a, 0, 3, SUB:P_END, :KVD] = q_kv[a, :, 0, :]
            pieces[a, 0, 3, SUB:P_END, KVD:LANES] = q_kv[a, :, 1, :]
            pieces[a, 1, 3, SUB:P_END, :] = q_up[a, :, 0, :LANES]
            pieces[a, 1, 0, TILE16:Q_END, :] = q_up[a, :, 0, LANES:FF]
            pieces[a, 1, 1, TILE16:Q_END, :] = q_up[a, :, 1, :LANES]
            pieces[a, 1, 2, TILE16:Q_END, :] = q_up[a, :, 1, LANES:FF]
            for xd in range(PAIR):
                for j in range(SLAB):
                    pieces[a, 0, xd, DOWN_AT + PAIR * j:DOWN_NEXT + PAIR * j, :] = q_dn[a, 0, :, LANES * j:LANES * j + LANES]

    acc[11] = jnp.zeros((RING, RING, BROWS, LANES), F32)

    @pl.when(core == 0)
    def _():
        acc[10] = jnp.zeros((RING, RING, BROWS, LANES), F32)

    pack_pieces()
    pl.semaphore_wait(barrier, PEERS)

    for k in range(RING):
        start_par(k)

    def pre(a, i):
        dx, dc = row_peers[i]
        return remote(pieces.at[a, (core, other)[dc], around["x"][dx]], recvp.at[a, slot], pre_s.at[a, i], pre_r.at[a, i], row_peer(dx, dc))

    def pre_start(a):
        for i in range(SLAB):
            pre(a, i).start()
        recvp[a, slot] = pieces[a, core, x]

    def pre_done(a):
        for i in range(SLAB):
            pre(a, i).wait_recv()
        for g in range(GROUPS):
            for s in range(SUB):
                mb[a, g, SLAB * s:SLAB * s + SLAB, :] = recvp[a, s, SUB * g:SUB * g + SLAB, :]

        @pl.when(jnp.logical_and(core == 0, x < 2))
        def _():
            for i in range(RING):
                for j in range(SLAB):
                    mb[a, 2, SUB * j + 2 * i:SUB * j + 2 * i + 2, :] = recvp[a, RING * x + i, DOWN_AT + PAIR * j:DOWN_NEXT + PAIR * j, :]

    pre_start(0)
    add_r(0)
    rs1[0]((0,))
    add_q(0)
    rs1[0]((2,))
    add_p(0)
    add_kv()
    rs1[0]((1,))
    for add, g in ((add_r, 0), (add_p, 1), (add_q, 2)):
        add(1)
        add(2)
        rs1[1]((g,))
    for add in (add_r, add_p, add_q):
        add(3)
    pre_done(0)

    ORDER = (2, 1, 0)
    for g in ORDER:
        rs1[2]((g,))
    for g in ORDER:
        rs1[3]((g,))
        rs2[0]((g,))
        rs2[1]((g,))
    for g in ORDER:
        rs2[2]((g,))
    for g in range(GROUPS):
        mg[RING * g + x, z, y] = mb[0, g]
    m3[0]()
    for g in ORDER:
        rs2[3]((g,))
        rs3[0]((g,))
    pre_start(1)
    for g in ORDER:
        rs3[1]((g,))
    m3[1]()
    for g in ORDER:
        for h in range(PAIR):
            grad = rs3[2](g, h) * (1.0 / GROUP)
            mom_new = MU * half3(mg, g, h)[...] + grad
            mt[g, 2 * h:2 * h + 2] = mom_new
            half3(xg, g, h)[...] = (grad + MU * mom_new).astype(BF16)
        u2[0]((g,))
    for g in range(GROUPS):
        nb[g] = mt[g, around[DIMS3[g]][0]]

    def pack_rows(src, dst):
        for s in range(SUB):
            for g in range(GROUPS):
                dst[s, SUB * g:SUB * g + SLAB, :] = src[g, SLAB * s:SLAB * s + SLAB, :]
            for j in range(SLAB):
                r = SUB * j + 2 * (s % RING)
                dst[s, DOWN_AT + PAIR * j:DOWN_NEXT + PAIR * j, :] = src[2, r:r + 2, :]

    def post(src, dst, ssem, rsem, i):
        dx, dc = row_peers[i]
        dest = row_slot[dx, dc]
        return remote(src.at[dest], dst.at[slot], ssem.at[i], rsem.at[i], row_peer(dx, dc))

    for g in ORDER:
        u2[1]((g,))
    pre_done(1)
    for g in range(GROUPS):
        wg[RING * g + x, z, y] = mb[1, g]
    wg3[0]()
    for g in ORDER:
        u2[2]((g,))
        u1[0]((g,))
    pack_rows(nb, outp)
    for g in ORDER:
        u1[1]((g,))
    for i in range(SLAB):
        post(outp, mrecv, mo_s, mo_r, i).start()
    mrecv[slot] = outp[slot]
    wg3[1]()
    wg2[0]()
    for g in ORDER:
        u1[2]((g,))

    def total(units):
        part = jnp.zeros((BROWS, LANES), F32)
        for u in units:
            v = xg[u].astype(F32)
            part = part + jnp.sum(v * v, axis=(0, 1))
        return 1.0 / (jnp.sqrt(jnp.sum(part, keepdims=True)) + EPS)

    def column(u, inv):
        return xg[u].astype(F32).reshape(D, LANES) * inv

    inv = total(range(SLAB))
    for u in range(SLAB):
        xx[0, :, LANES * u:LANES * u + LANES] = column(u, inv).astype(BF16)

    @pl.when(core == 0)
    def _():
        inv_d = total((SUB, 9))
        both = [(xg[u].astype(F32) * inv_d).reshape(TILE16, SLAB, SUB, LANES) for u in (SUB, 9)]
        both = jnp.concatenate(both, axis=2)
        for j in range(SLAB):
            ss[0, 0, :, LANES * j:LANES * j + LANES] = both[:, j].reshape(FF, LANES).astype(BF16)
        v = xg[SLAB].astype(F32)
        v = v.reshape(D, LANES).T
        for i in range(PAIR):
            h = v[KVD * i:KVD * i + KVD]
            norm = jnp.sqrt(jnp.sum(h * h, keepdims=True))
            ss[0, 1, KVD * i:KVD * i + KVD, :] = (h * (1.0 / (norm + EPS))).astype(BF16)
        ss[0, 1, LANES:FF, :] = jnp.zeros((LANES, D), BF16)

    @pl.when(core == 1)
    def _():
        for i in range(PAIR):
            inv_u = total((SLAB + 2 * i, SUB + 2 * i))
            for h in range(PAIR):
                ss[0, i, LANES * h:LANES * h + LANES, :] = column(SLAB + 2 * i + h, inv_u).T.astype(BF16)

    wg2[1]()

    NT = (((1,), (1,)), ((), ()))
    ROWS = ((0, FF), (FF, FF), (HALF_D, FF), (TAIL_D, LANES))
    row_id = lax.broadcasted_iota(jnp.int32, (FF, FF), 0) // KVD
    col_id = lax.broadcasted_iota(jnp.int32, (FF, FF), 1) // KVD
    keep = jnp.logical_or(row_id == col_id, core == 1)

    def symmetric(product, out):
        for r in (0, FF, HALF_D):
            value = product(r, FF, r, TAIL_D - r)
            out[r:r + FF, r:TAIL_D] = value
            if r < HALF_D:
                out[r + FF:TAIL_D, r:r + FF] = value[:, FF:].T
        value = product(TAIL_D, LANES, 0, D)
        out[TAIL_D:D, :] = value
        out[:TAIL_D, TAIL_D:D] = value[:, :TAIL_D].T

    def poly_step(cur, it):
        def gram(r, n, c, m):
            return lax.dot_general(xx[cur, r:r + n, :], xx[cur, c:c + m, :], NT, preferred_element_type=F32).astype(BF16)

        symmetric(gram, aa)
        for i in range(PAIR):
            g = lax.dot_general(ss[cur, i], ss[cur, i], NT, preferred_element_type=F32)
            if i == 1:
                g = jnp.where(keep, g, 0.0)
            sa[i] = g.astype(BF16)

        if it == 0:
            wg2[2]()
            wg1[0]()
        if it == 2:
            wg1[1]()

        def poly(r, n, c, m):
            sq = jnp.dot(aa[r:r + n, :], aa[:, c:c + m], preferred_element_type=F32)
            return (COEF_B * aa[r:r + n, c:c + m].astype(F32) + COEF_C * sq).astype(BF16)

        symmetric(poly, bb)
        for i in range(PAIR):
            sq = jnp.dot(sa[i], sa[i], preferred_element_type=F32)
            sb[i] = (COEF_B * sa[i].astype(F32) + COEF_C * sq).astype(BF16)

    def apply_small(cur, nxt):
        for i in range(PAIR):
            prod = jnp.dot(sb[i], ss[cur, i], preferred_element_type=F32)
            ss[nxt, i] = (COEF_A * ss[cur, i].astype(F32) + prod).astype(BF16)

    def apply_rows(cur, r, n):
        prod = jnp.dot(bb[pl.ds(r, n), :], xx[cur], preferred_element_type=F32)
        return (COEF_A * xx[cur, pl.ds(r, n), :].astype(F32) + prod).astype(BF16)

    def step(it, carry):
        cur = it % 2
        nxt = 1 - cur
        poly_step(cur, it)
        for r, n in ROWS:
            xx[nxt, r:r + n, :] = apply_rows(cur, r, n)
        apply_small(cur, nxt)
        return carry

    for it in range(NS_STEPS - 1):
        step(it, 0)
    cur = (NS_STEPS - 1) % 2
    fin = 1 - cur
    poly_step(cur, None)
    apply_small(cur, fin)

    wg1[2]()
    wg1[3]()
    wg2[3]()
    wg3[2]()

    def update(w, v):
        return w - LR * (SCALE * v + WD * w)

    def out_copy(i, ref):
        return remote(ref, ref, or_s.at[i], or_r.at[i], partner)

    def sq_ref(p, c):
        return vb_sq.at[c, pl.ds(pl.multiple_of(QROWS * p, ALIGN), QROWS)]

    def small_refs(c):
        return (vb_kv, vb_dn) if c == 0 else (vb_up.at[0], vb_up.at[1])

    def column_new(u, v):
        new = update(wg[u].reshape(D, LANES), v)
        wg[u] = new.reshape(RING, RING, BROWS, LANES)
        return new

    @pl.when(core == 0)
    def _():
        v = ss[fin, 1, :LANES, :].astype(F32).T
        vb_kv[...] = column_new(SLAB, v).T.astype(BF16)
        for j in range(SLAB):
            v = ss[fin, 0, :, LANES * j:LANES * j + LANES].astype(F32).reshape(RING, RING, TILE16, LANES)
            lo = update(wg[SUB, :, :, SUB * j:SUB * j + SUB, :], v[:, :, :SUB])
            hi = update(wg[9, :, :, SUB * j:SUB * j + SUB, :], v[:, :, SUB:TILE16])
            wg[SUB, :, :, SUB * j:SUB * j + SUB, :] = lo
            wg[9, :, :, SUB * j:SUB * j + SUB, :] = hi
            vb_dn[:, LANES * j:LANES * j + LANES] = jnp.concatenate([lo, hi], axis=2).reshape(FF, LANES).astype(BF16)
        for i in range(PAIR):
            out_copy(SUB + i, small_refs(0)[i]).start()

    @pl.when(core == 1)
    def _():
        for i in range(PAIR):
            for h in range(PAIR):
                v = ss[fin, i, LANES * h:LANES * h + LANES, :].astype(F32).T
                vb_up[i, :, LANES * h:LANES * h + LANES] = column_new(SLAB + 2 * i + h, v).astype(BF16)
        for i in range(PAIR):
            out_copy(SUB + i, small_refs(1)[i]).start()

    for i in range(RING):
        q = around["z"][i]
        v = apply_rows(cur, pl.multiple_of(QROWS * q, ALIGN), QROWS).astype(F32)
        for u in range(SLAB):
            new = update(wg[u, q].reshape(QROWS, LANES), v[:, LANES * u:LANES * u + LANES])
            wg[u, q] = new.reshape(RING, BROWS, LANES)
            vb_sq[core, pl.ds(pl.multiple_of(QROWS * q, ALIGN), QROWS), LANES * u:LANES * u + LANES] = new.astype(BF16)
        out_copy(i, sq_ref(q, core)).start()
        if i == 0:
            for g in range(GROUPS):
                nb[g] = wg[RING * g + x, z, y]
            pack_rows(nb, outw)
            for k in range(SLAB):
                post(outw, wrecv, wo_s, wo_r, k).start()
            wrecv[slot] = outw[slot]

    for i in range(SLAB):
        post(outp, mrecv, mo_s, mo_r, i).wait_recv()
        post(outw, wrecv, wo_s, wo_r, i).wait_recv()

    for p in range(RING):
        out_copy(p, sq_ref(around["z"][p], core)).wait()
    for c in range(PAIR):
        @pl.when(core == c)
        def _():
            for i in range(PAIR):
                out_copy(SUB + i, small_refs(c)[i]).wait_send()
                out_copy(SUB + i, small_refs(1 - c)[i]).wait_recv()
    for i in range(SLAB):
        pre(0, i).wait_send()
        pre(1, i).wait_send()
        post(outp, mrecv, mo_s, mo_r, i).wait_send()
        post(outw, wrecv, wo_s, wo_r, i).wait_send()
    for k in range(RING):
        for i, item in enumerate(common_items(other, k, 1)):
            par_copy(k, i, item).wait_send()
        for tc in range(PAIR):
            @pl.when(core == 1 - tc)
            def _():
                for i, item in enumerate(special_items(tc, k, 1)):
                    par_copy(k, 2 + i, item).wait_send()
    rs1[RING]()
    rs2[RING]()
    rs3[3]()
    m3[2]()
    u2[3]()
    u1[3]()


def unpack_rows(slot, src, o_sq, o_kv, o_up, o_dn):
    for c in range(PAIR):
        for xs in range(RING):
            t = 2 * xs + c
            o_sq[:, c, LANES * xs:LANES * xs + LANES] = src[t, :SLAB, :]
            if xs < 3:
                o_sq[:, c, HALF_D + LANES * xs:P_AT + LANES * xs] = src[t, SUB:P_END, :]
    o_kv[:, 0, :] = src[HOPS, SUB:P_END, :KVD]
    o_kv[:, 1, :] = src[HOPS, SUB:P_END, KVD:LANES]
    o_up[:, 0, :LANES] = src[SLAB, SUB:P_END, :]
    o_up[:, 0, LANES:FF] = src[1, TILE16:Q_END, :]
    o_up[:, 1, :LANES] = src[3, TILE16:Q_END, :]
    o_up[:, 1, LANES:FF] = src[5, TILE16:Q_END, :]
    t = 2 * lax.div(slot, RING)
    for j in range(SLAB):
        o_dn[0, :, LANES * j:LANES * j + LANES] = src[t, DOWN_AT + PAIR * j:DOWN_NEXT + PAIR * j, :]


def write_out(
    mrecv, wrecv, vb_sq, vb_kv, vb_up, vb_dn,
    mo_sq, mo_kv, mo_up, mo_dn, wo_sq, wo_kv, wo_up, wo_dn, b_sq, b_kv, b_up, b_dn, sem,
):
    copies = [pltpu.make_async_copy(src, dst, sem.at[i]) for i, (src, dst) in enumerate(
        ((vb_sq, b_sq), (vb_kv, b_kv), (vb_up, b_up), (vb_dn, b_dn)))]
    for cp in copies:
        cp.start()
    me = lax.axis_index("data")
    slot = lax.rem(me, SUB)
    unpack_rows(slot, mrecv, mo_sq, mo_kv, mo_up, mo_dn)
    unpack_rows(slot, wrecv, wo_sq, wo_kv, wo_up, wo_dn)
    for cp in copies:
        cp.wait()


def solution(mesh):
    grad_spec = P(("model", "data"))
    slab_spec = P("model", "data")
    full_spec = P("model")

    def local_step(g_sq, m_sq, w_sq, g_kv, m_kv, w_kv, g_up, m_up, w_up, g_dn, m_dn, w_dn):
        g_sq = g_sq.reshape(2, RING, RING, BROWS, D)
        g_kv = g_kv[0].transpose(0, 2, 1)
        g_up = g_up.reshape(2, RING, RING, BROWS, FF)
        g_dn = g_dn.reshape(RING, RING, TILE16, D)
        vm = pl.BlockSpec(memory_space=pltpu.VMEM)
        hb = pl.BlockSpec(memory_space=pltpu.HBM)
        V = pltpu.VMEM
        block = (BROWS, LANES)
        unit = (RING, RING) + block
        half = (PAIR, RING) + block
        two = (PAIR,) + block
        mats = (PAIR, PAIR)
        rows_of = (PAIR, SLAB, PAIR)
        floats = [
            (PAIR, RING) + unit, (PAIR, RING, RING, BROWS, TRIO), mats + (KVD, D), mats + (RING, RING, BROWS, FF), (PAIR, RING, RING, TILE16, D), (UNITS,) + unit,
            (HOPS,) + half, (HOPS,) + half, (HOPS, GROUPS) + two, (GROUPS, HOPS) + two, (GROUPS,) + mats + two, (GROUPS, PAIR) + two,
            (UNITS,) + unit, (GROUPS, RING) + block,
            rows_of + (D,), rows_of + (KVD,), rows_of + (FF,), (2, 1, 2, D),
            mats + (RING, PACK, LANES), (PAIR, SUB, PACK, LANES), (PAIR, GROUPS) + block, (GROUPS,) + block, PACKED, PACKED,
        ]
        scratch = [V(a, F32) for a in floats] + [V((UNITS,) + unit, BF16), V((UNITS,) + unit, F32)]
        scratch += [V(a, BF16) for a in ((PAIR, D, D), (D, D), (D, D), mats + (FF, D), (PAIR, FF, FF), (PAIR, FF, FF))]
        ring, pairs, direct, row = (GROUPS, HOPS), (GROUPS, RING), (GROUPS, GROUPS), (SLAB,)
        sems = [(RING, 5), (2, RING)]
        for a in ((RING, 5), (PAIR,) + row, row, row, ring, ring, pairs, direct, ring, ring, direct, ring, ring, (10,)):
            sems += [a, a]
        scratch += [DMA(a) for a in sems]

        def rows(a):
            return a.transpose(1, 0, 2)

        mid = [V(s, F32) for s in (PACKED, PACKED)]
        mid += [V(s, BF16) for s in ((2, D, D), (LANES, D), (2, D, FF), (FF, D))]
        parts = pl.pallas_call(
            kernel,
            out_shape=mid,
            in_specs=[hb] * UNITS,
            out_specs=[vm] * HOPS,
            scratch_shapes=scratch,
            compiler_params=pltpu.CompilerParams(collective_id=0, has_side_effects=True, vmem_limit_bytes=61700000),
            name="muon",
        )(g_sq, g_kv, g_up, g_dn, rows(m_sq), rows(m_kv), rows(m_up), m_dn, rows(w_sq), rows(w_kv), rows(w_up), w_dn)
        small = [jax.ShapeDtypeStruct(s, F32) for s in ((SLAB, PAIR, D), (SLAB, PAIR, KVD), (SLAB, PAIR, FF), (1, PAIR, D))]
        full = [jax.ShapeDtypeStruct(s, BF16) for s in ((2, D, D), (LANES, D), (2, D, FF), (FF, D))]
        out = pl.pallas_call(
            write_out,
            out_shape=small + small + full,
            in_specs=[vm] * HOPS,
            out_specs=[vm] * SUB + [hb] * RING,
            scratch_shapes=[DMA((RING,))],
            compiler_params=pltpu.CompilerParams(vmem_limit_bytes=4_000_000),
            name="write_out",
        )(*parts)
        m, w, b = out[0:RING], out[RING:SUB], out[SUB:UNITS]
        return (
            rows(m[0]), rows(w[0]), b[0],
            rows(m[1]), rows(w[1]), b[1].reshape(2, KVD, D).transpose(0, 2, 1),
            rows(m[2]), rows(w[2]), b[2],
            m[3], w[3], b[3].reshape(1, FF, D),
        )

    in_specs = (grad_spec, slab_spec, slab_spec) * RING
    out_specs = (slab_spec, slab_spec, full_spec) * RING
    return jax.shard_map(local_step, mesh=mesh, in_specs=in_specs, out_specs=out_specs, check_vma=False)
```

time: 103 us -> 103 us (level)
  no operation moved by 1% of the time
where the time goes in v4:
time: 103 us
  Pallas kernels  102 us (99%)
    pallas_call x1, Pallas kernels, local_step(): pl.pallas_call(kernel, out_shape=mid, in_specs=[hb] * UNITS, out_specs=[v...  99.6 us
    pallas_call x1, Pallas kernels, local_step(): pl.pallas_call(write_out, out_shape=small + small + full, in_specs=[vm] *...  2.91 us

profile of v4, /device:TPU:1, one launch (start us, length us, event | category | flops | bytes accessed | tf_op | source)
XLA Modules:
  0.0 103.3 jit_solution(6567337787657127210)
XLA Ops:
  0.6 99.6 %muon.1 = (f32[8,40,128]{2,1,0:T(8,128)S(1)}, f32[8,40,128]{2,1,0:T(8,128)S(1)}, bf16[2,896,896]{2,1,0:T(8,128)(2,1)S(1)}, bf16[128,896]{1,0:T(8,128)(2,1)S(1)},...) custom-call(f32[2,4,4,56,896]{4,3,2,1,0:T(8,128)} %bitcast.22, f32[2,64,896]{2,1,0:T(8,128)} %bitcast.25, ...), custom_call_target="tpu_custom_call" | custom-call | tf_op jit(solution)/shard_map/muon/pallas_call | solution.py:790
  100.2 2.9 %write_out.1 = (f32[7,2,896]{2,1,0:T(2,128)}, f32[7,2,64]{2,1,0:T(2,128)}, f32[7,2,256]{2,1,0:T(2,128)}, f32[1,2,896]{2,1,0:T(2,128)}, f32[7,2,896]{2,1,0:T(2,12...) custom-call(f32[8,40,128]{2,1,0:T(8,128)S(1)} %get-tuple-element.30., ...), custom_call_target="tpu_custom_call" | custom-call | tf_op jit(solution)/shard_map/write_out/pallas_call | solution.py:801

commit v5 on v4

--- a/solution.py
+++ b/solution.py
@@ -55,7 +55,7 @@
     w_sq, w_kv, w_up, w_dn,
     mrecv, wrecv, vb_sq, vb_kv, vb_up, vb_dn,
     br, bp, kvb, upb, dnb, acc,
-    r1a, r1b, r1c, r2, r3, s3, mg, mt,
+    r1, r2, r3, s3, mg, mt,
     q_sq, q_kv, q_up, q_dn,
     pieces, recvp, mb, nb, outp, outw,
     xg, wg, xx, aa, bb, ss, sa, sb,
@@ -222,6 +222,17 @@
             return buf.at[RING + j, z, pl.ds(PAIR * h, PAIR)]
         return buf.at[pl.ds(SUB + PAIR * h, PAIR), j, y]
 
+    def piece(d2):
+        def half(buf, grp, j1, h):
+            j2 = around[DIMS2[grp]][d2]
+            if grp == 0:
+                return buf.at[j1, pl.ds(PAIR * h, PAIR), j2]
+            if grp == 1:
+                return buf.at[RING + j2, j1, pl.ds(PAIR * h, PAIR)]
+            return buf.at[pl.ds(SUB + PAIR * h, PAIR), j2, j1]
+
+        return half
+
     def half3(buf, grp, h):
         if grp == 0:
             return buf.at[x, pl.ds(PAIR * h, PAIR), y]
@@ -296,17 +307,20 @@
                 desc(grp, 3).wait_recv()
                 desc(grp, 5).start()
 
+        def arrived(grp, which):
+            for i in which:
+                desc(grp, i).wait_recv()
+
         def last(groups=ALL):
             for grp in groups:
-                for i in (1, RING, 2, 5):
-                    desc(grp, i).wait_recv()
+                arrived(grp, (1, RING, PAIR, 5))
 
         def drain():
             for grp in range(GROUPS):
                 for i in range(HOPS):
                     desc(grp, i).wait_send()
 
-        return first, second, last, drain
+        return first, second, last, drain, arrived
 
     swap = {}
     for d in "xyz":
@@ -364,12 +378,12 @@
 
         return first, last, drain
 
-    rs1 = rs_ring(half1, acc, DIMS1, (r1a, r1b, r1c), rs1_s, rs1_r)
+    rs1 = [rs_ring(piece(OFFS[k]), acc, DIMS1, [r1.at[k, g] for g in ALL], rs1_s.at[k], rs1_r.at[k]) for k in range(RING)]
     rs2 = rs_ring(half2, acc, DIMS2, (r2.at[0], r2.at[1], r2.at[2]), rs2_s, rs2_r)
     rs3 = sum_pairs()
     m3 = ag_direct(mg, m3_s, m3_r)
     u2 = ag_ring(half2, xg, DIMS2, u2_s, u2_r)
-    u1 = ag_ring(half1, xg, DIMS1, u1_s, u1_r)
+    u1 = [ag_ring(piece(d), xg, DIMS1, u1_s.at[d], u1_r.at[d]) for d in range(RING)]
     wg3 = ag_direct(wg, w3_s, w3_r)
     wg2 = ag_ring(half2, wg, DIMS2, w2_s, w2_r)
     wg1 = ag_ring(half1, wg, DIMS1, w1_s, w1_r)
@@ -437,31 +451,45 @@
                 for j in range(SLAB):
                     mb[a, 2, SUB * j + 2 * i:SUB * j + 2 * i + 2, :] = recvp[a, RING * x + i, DOWN_AT + PAIR * j:DOWN_NEXT + PAIR * j, :]
 
+    ORDER = (2, 1, 0)
     pre_start(0)
-    add_r(0)
-    rs1[0]((0,))
-    add_q(0)
-    rs1[0]((2,))
-    add_p(0)
-    add_kv()
-    rs1[0]((1,))
-    for add, g in ((add_r, 0), (add_p, 1), (add_q, 2)):
+    for add, g in ((add_r, 0), (add_q, PAIR), (add_p, 1)):
+        add(0)
+        if g == 1:
+            add_kv()
+        for k in range(RING):
+            rs1[k][0]((g,))
+    for add, g in ((add_r, 0), (add_p, 1), (add_q, PAIR)):
         add(1)
-        add(2)
-        rs1[1]((g,))
+        add(PAIR)
+        rs1[0][1]((g,))
     for add in (add_r, add_p, add_q):
-        add(3)
+        add(GROUPS)
+    def forward(k):
+        for g in ORDER:
+            if k:
+                rs1[k][1]((g,))
+            rs1[k][2]((g,))
+
+    def finish(k):
+        for g in ORDER:
+            rs1[k][GROUPS]((g,))
+            if k == 0:
+                rs2[0]((g,))
+            if k == 2:
+                rs2[1]((g,))
+
+    forward(0)
+    forward(1)
+    finish(0)
+    forward(2)
+    finish(1)
+    forward(GROUPS)
     pre_done(0)
-
-    ORDER = (2, 1, 0)
-    for g in ORDER:
-        rs1[2]((g,))
-    for g in ORDER:
-        rs1[3]((g,))
-        rs2[0]((g,))
-        rs2[1]((g,))
+    finish(2)
     for g in ORDER:
         rs2[2]((g,))
+    finish(GROUPS)
     for g in range(GROUPS):
         mg[RING * g + x, z, y] = mb[0, g]
     m3[0]()
@@ -479,6 +507,8 @@
             mt[g, 2 * h:2 * h + 2] = mom_new
             half3(xg, g, h)[...] = (grad + MU * mom_new).astype(BF16)
         u2[0]((g,))
+    for g in ORDER:
+        u1[0][0]((g,))
     for g in range(GROUPS):
         nb[g] = mt[g, around[DIMS3[g]][0]]
 
@@ -497,23 +527,32 @@
 
     for g in ORDER:
         u2[1]((g,))
+    for g in ORDER:
+        u2[RING](g, (1, RING))
+        u1[GROUPS][0]((g,))
+        u1[1][0]((g,))
+    for g in ORDER:
+        u1[0][1]((g,))
     pre_done(1)
     for g in range(GROUPS):
         wg[RING * g + x, z, y] = mb[1, g]
+    for g in ORDER:
+        u2[RING](g, (PAIR, 5))
+        u1[PAIR][0]((g,))
     wg3[0]()
     for g in ORDER:
-        u2[2]((g,))
-        u1[0]((g,))
+        u1[GROUPS][1]((g,))
+        u1[1][1]((g,))
     pack_rows(nb, outp)
     for g in ORDER:
-        u1[1]((g,))
+        u1[PAIR][1]((g,))
     for i in range(SLAB):
         post(outp, mrecv, mo_s, mo_r, i).start()
     mrecv[slot] = outp[slot]
     wg3[1]()
     wg2[0]()
-    for g in ORDER:
-        u1[2]((g,))
+    for d in (0, GROUPS, 1, PAIR):
+        u1[d][2]()
 
     def total(units):
         part = jnp.zeros((BROWS, LANES), F32)
@@ -551,7 +590,6 @@
             for h in range(PAIR):
                 ss[0, i, LANES * h:LANES * h + LANES, :] = column(SLAB + 2 * i + h, inv_u).T.astype(BF16)
 
-    wg2[1]()
 
     NT = (((1,), (1,)), ((), ()))
     ROWS = ((0, FF), (FF, FF), (HALF_D, FF), (TAIL_D, LANES))
@@ -581,10 +619,10 @@
             sa[i] = g.astype(BF16)
 
         if it == 0:
+            wg2[1]()
+        if it == 1:
             wg2[2]()
             wg1[0]()
-        if it == 2:
-            wg1[1]()
 
         def poly(r, n, c, m):
             sq = jnp.dot(aa[r:r + n, :], aa[:, c:c + m], preferred_element_type=F32)
@@ -594,6 +632,8 @@
         for i in range(PAIR):
             sq = jnp.dot(sa[i], sa[i], preferred_element_type=F32)
             sb[i] = (COEF_B * sa[i].astype(F32) + COEF_C * sq).astype(BF16)
+        if it == 2:
+            wg1[1]()
 
     def apply_small(cur, nxt):
         for i in range(PAIR):
@@ -706,12 +746,13 @@
             def _():
                 for i, item in enumerate(special_items(tc, k, 1)):
                     par_copy(k, 2 + i, item).wait_send()
-    rs1[RING]()
+    for k in range(RING):
+        rs1[k][RING]()
+        u1[k][GROUPS]()
     rs2[RING]()
     rs3[3]()
     m3[2]()
     u2[3]()
-    u1[3]()
 
 
 def unpack_rows(slot, src, o_sq, o_kv, o_up, o_dn):
@@ -769,16 +810,16 @@
         rows_of = (PAIR, SLAB, PAIR)
         floats = [
             (PAIR, RING) + unit, (PAIR, RING, RING, BROWS, TRIO), mats + (KVD, D), mats + (RING, RING, BROWS, FF), (PAIR, RING, RING, TILE16, D), (UNITS,) + unit,
-            (HOPS,) + half, (HOPS,) + half, (HOPS, GROUPS) + two, (GROUPS, HOPS) + two, (GROUPS,) + mats + two, (GROUPS, PAIR) + two,
+            (RING, GROUPS, HOPS) + two, (GROUPS, HOPS) + two, (GROUPS,) + mats + two, (GROUPS, PAIR) + two,
             (UNITS,) + unit, (GROUPS, RING) + block,
             rows_of + (D,), rows_of + (KVD,), rows_of + (FF,), (2, 1, 2, D),
             mats + (RING, PACK, LANES), (PAIR, SUB, PACK, LANES), (PAIR, GROUPS) + block, (GROUPS,) + block, PACKED, PACKED,
         ]
         scratch = [V(a, F32) for a in floats] + [V((UNITS,) + unit, BF16), V((UNITS,) + unit, F32)]
         scratch += [V(a, BF16) for a in ((PAIR, D, D), (D, D), (D, D), mats + (FF, D), (PAIR, FF, FF), (PAIR, FF, FF))]
-        ring, pairs, direct, row = (GROUPS, HOPS), (GROUPS, RING), (GROUPS, GROUPS), (SLAB,)
+        rings, ring, pairs, direct, row = (RING, GROUPS, HOPS), (GROUPS, HOPS), (GROUPS, RING), (GROUPS, GROUPS), (SLAB,)
         sems = [(RING, 5), (2, RING)]
-        for a in ((RING, 5), (PAIR,) + row, row, row, ring, ring, pairs, direct, ring, ring, direct, ring, ring, (10,)):
+        for a in ((RING, 5), (PAIR,) + row, row, row, rings, ring, pairs, direct, ring, rings, direct, ring, ring, (10,)):
             sems += [a, a]
         scratch += [DMA(a) for a in sems]
 

time: 103 us -> 99.7 us (0.968)
  Pallas kernels: 102 us -> 98.7 us
    pallas_call x1, Pallas kernels: 99.6 us -> 95.8 us  [local_step(): pl.pallas_call(kernel, out_shape=mid, in_specs=[hb] * UNITS, out_specs=[v...]
where the time goes in v5:
time: 99.7 us; the launch traced here: 99.5 us
  Pallas kernels  98.7 us (99%)
    pallas_call x1, Pallas kernels, local_step(): pl.pallas_call(kernel, out_shape=mid, in_specs=[hb] * UNITS, out_specs=[v...  95.8 us
    pallas_call x1, Pallas kernels, local_step(): pl.pallas_call(write_out, out_shape=small + small + full, in_specs=[vm] *...  2.91 us

profile of v5, /device:TPU:1, one launch (start us, length us, event | category | flops | bytes accessed | tf_op | source)
XLA Modules:
  0.0 99.5 jit_solution(4022807935073530619)
XLA Ops:
  0.6 95.8 %muon.1 = (f32[8,40,128]{2,1,0:T(8,128)S(1)}, f32[8,40,128]{2,1,0:T(8,128)S(1)}, bf16[2,896,896]{2,1,0:T(8,128)(2,1)S(1)}, bf16[128,896]{1,0:T(8,128)(2,1)S(1)},...) custom-call(f32[2,4,4,56,896]{4,3,2,1,0:T(8,128)} %bitcast.22, f32[2,64,896]{2,1,0:T(8,128)} %bitcast.25, ...), custom_call_target="tpu_custom_call" | custom-call | tf_op jit(solution)/shard_map/muon/pallas_call | solution.py:831
  96.4 2.9 %write_out.1 = (f32[7,2,896]{2,1,0:T(2,128)}, f32[7,2,64]{2,1,0:T(2,128)}, f32[7,2,256]{2,1,0:T(2,128)}, f32[1,2,896]{2,1,0:T(2,128)}, f32[7,2,896]{2,1,0:T(2,12...) custom-call(f32[8,40,128]{2,1,0:T(8,128)S(1)} %get-tuple-element.30., ...), custom_call_target="tpu_custom_call" | custom-call | tf_op jit(solution)/shard_map/write_out/pallas_call | solution.py:842

commit v6 on v5

--- a/solution.py
+++ b/solution.py
@@ -775,16 +775,21 @@
 
 def write_out(
     mrecv, wrecv, vb_sq, vb_kv, vb_up, vb_dn,
-    mo_sq, mo_kv, mo_up, mo_dn, wo_sq, wo_kv, wo_up, wo_dn, b_sq, b_kv, b_up, b_dn, sem,
+    mo_sq, mo_kv, mo_up, mo_dn, wo_sq, wo_kv, wo_up, wo_dn, b_sq, b_kv, b_up, b_dn, *scratch,
 ):
+    sem, stage = scratch[-1], scratch[:-1]
     copies = [pltpu.make_async_copy(src, dst, sem.at[i]) for i, (src, dst) in enumerate(
         ((vb_sq, b_sq), (vb_kv, b_kv), (vb_up, b_up), (vb_dn, b_dn)))]
     for cp in copies:
         cp.start()
     me = lax.axis_index("data")
     slot = lax.rem(me, SUB)
-    unpack_rows(slot, mrecv, mo_sq, mo_kv, mo_up, mo_dn)
-    unpack_rows(slot, wrecv, wo_sq, wo_kv, wo_up, wo_dn)
+    for at, src, outs in ((0, mrecv, (mo_sq, mo_kv, mo_up, mo_dn)), (RING, wrecv, (wo_sq, wo_kv, wo_up, wo_dn))):
+        bufs = stage[at:at + RING]
+        unpack_rows(slot, src, *bufs)
+        for i, out in enumerate(outs):
+            copies.append(pltpu.make_async_copy(bufs[i], out, sem.at[RING + at + i]))
+            copies[-1].start()
     for cp in copies:
         cp.wait()
 
@@ -843,8 +848,8 @@
             write_out,
             out_shape=small + small + full,
             in_specs=[vm] * HOPS,
-            out_specs=[vm] * SUB + [hb] * RING,
-            scratch_shapes=[DMA((RING,))],
+            out_specs=[hb] * UNITS,
+            scratch_shapes=[V(a.shape, F32) for a in small + small] + [DMA((UNITS,))],
             compiler_params=pltpu.CompilerParams(vmem_limit_bytes=4_000_000),
             name="write_out",
         )(*parts)

time: 99.7 us -> 99.2 us (level)
  no operation moved by 1% of the time
where the time goes in v6:
time: 99.2 us; the launch traced here: 99 us
  Pallas kernels  98.2 us (99%)
    pallas_call x1, Pallas kernels, local_step(): pl.pallas_call(kernel, out_shape=mid, in_specs=[hb] * UNITS, out_specs=[v...  95.8 us
    pallas_call x1, Pallas kernels, local_step(): pl.pallas_call(write_out, out_shape=small + small + full, in_specs=[vm] *...  2.42 us

profile of v6, /device:TPU:1, one launch (start us, length us, event | category | flops | bytes accessed | tf_op | source)
XLA Modules:
  0.0 99.0 jit_solution(17552725207917881926)
XLA Ops:
  0.6 95.8 %muon.1 = (f32[8,40,128]{2,1,0:T(8,128)S(1)}, f32[8,40,128]{2,1,0:T(8,128)S(1)}, bf16[2,896,896]{2,1,0:T(8,128)(2,1)S(1)}, bf16[128,896]{1,0:T(8,128)(2,1)S(1)},...) custom-call(f32[2,4,4,56,896]{4,3,2,1,0:T(8,128)} %bitcast.22, f32[2,64,896]{2,1,0:T(8,128)} %bitcast.25, ...), custom_call_target="tpu_custom_call" | custom-call | tf_op jit(solution)/shard_map/muon/pallas_call | solution.py:836
  96.4 2.4 %write_out.1 = (f32[7,2,896]{2,1,0:T(2,128)}, f32[7,2,64]{2,1,0:T(2,128)}, f32[7,2,256]{2,1,0:T(2,128)}, f32[1,2,896]{2,1,0:T(2,128)}, f32[7,2,896]{2,1,0:T(2,12...) custom-call(f32[8,40,128]{2,1,0:T(8,128)S(1)} %get-tuple-element.30., ...), custom_call_target="tpu_custom_call" | custom-call | tf_op jit(solution)/shard_map/write_out/pallas_call | solution.py:847
